TPU v7x, 32 devices: a whole 2x2x4 slice. The times are simulated.
32 devices in a mesh: grp: 1, sp: 32 (over z, y, x, core), ch: 1.
Axes of the slice: x: 2, y: 2, z: 4, core: 2. Of those that a mesh axis runs over, the one named last changes fastest.
Arguments:
- latents: bfloat16 [131072, 1024], P(('grp', 'sp')), may hold values from -6 to 6
- spectrum: bfloat16 [16, 64, 128, 1024], P(None, None, 'sp', 'ch'), may hold values from -4 to 4
- w_value: bfloat16 [1024, 1024], P('sp', 'ch'), may hold values from -0.1875 to 0.1875
- w_gate: bfloat16 [1024, 1024], P('sp', 'ch'), may hold values from -0.1875 to 0.1875
- w_out: bfloat16 [1024, 1024], P('sp'), may hold values from -0.1875 to 0.1875
- embed_table: bfloat16 [1024, 32768], P(('sp', 'ch')), may hold values from -12 to 12
- prompt_ids: int32 [256], P('grp'), may hold values from 0 to 32767
- noise_step: int32 [1], P('grp'), may hold values from 0 to 999
Outputs:
- denoised: bfloat16 [131072, 1024], P(('grp', 'sp', 'ch'))
All inputs are finite; a program needn't handle non-finite values.
Results may differ from a plain program's by a relative error of at most 0.013.
Values may be sent and summed in bfloat16 or wider, within the bound.
No kernel may reach another device: no remote copies, remote signals or barrier semaphores. Data moves between devices by JAX's collectives and lax.ppermute only.
A program may use at most 128 MiB of HBM per device.

v0:
```python
import math

import jax
import jax.numpy as jnp
from jax import lax
from jax.sharding import PartitionSpec as P

TT = 16
HH = 64
WW = 128
C = 1024


def cas_table(length):
    position = jnp.arange(length, dtype=jnp.int32)
    product = position[:, None] * position[None, :] % length
    phase_angle = product.astype(jnp.float32) * (2.0 * math.pi / length)
    return ((jnp.cos(phase_angle) + jnp.sin(phase_angle)) / math.sqrt(length)).astype(jnp.bfloat16)


def step_embedding(noise_step, channel, channels):
    half_count = channels // 2
    lower_half = channel < half_count
    position = jnp.where(lower_half, channel, channel - half_count).astype(jnp.float32)
    frequency = jnp.exp(-math.log(10000.0) * position / half_count)
    phase_angle = noise_step[0].astype(jnp.float32) * frequency
    return jnp.where(lower_half, jnp.sin(phase_angle), jnp.cos(phase_angle))


def apply_table(form, table, operand):
    return jnp.einsum(form, table, operand, preferred_element_type=jnp.float32)


def local(latents, spectrum, w_value, w_gate, w_out, embed_table, prompt_ids, noise_step):
    row_count = latents.shape[0]
    chan_part = w_value.shape[1]
    full_value, full_gate, full_out = (
        lax.all_gather(w_value, "sp", axis=0, tiled=True),
        lax.all_gather(w_gate, "sp", axis=0, tiled=True),
        lax.all_gather(w_out, "sp", axis=0, tiled=True),
    )
    value_rows = jnp.dot(latents, full_value, preferred_element_type=jnp.float32).astype(
        jnp.bfloat16
    )
    gate_rows = jnp.dot(latents, full_gate, preferred_element_type=jnp.float32)
    cas_width = cas_table(WW)
    cas_height = cas_table(HH)
    cas_time = cas_table(TT)
    line_grid = value_rows.reshape(row_count // WW, WW, chan_part)
    width_spec = apply_table("kw,lwc->lkc", cas_width, line_grid).astype(jnp.bfloat16)
    pencil = lax.all_to_all(width_spec, "sp", split_axis=1, concat_axis=0, tiled=True)
    band_count = pencil.shape[1]
    pencil = pencil.reshape(TT, HH, band_count, chan_part)
    height_spec = apply_table("ah,thkc->takc", cas_height, pencil).astype(jnp.bfloat16)
    full_spec = apply_table("st,takc->sakc", cas_time, height_spec).astype(jnp.bfloat16)
    filtered = (full_spec.astype(jnp.float32) * spectrum.astype(jnp.float32)).astype(jnp.bfloat16)
    time_back = apply_table("ts,sakc->takc", cas_time, filtered).astype(jnp.bfloat16)
    height_back = apply_table("ha,takc->thkc", cas_height, time_back).astype(jnp.bfloat16)
    returned = lax.all_to_all(
        height_back.reshape(TT * HH, band_count, chan_part),
        "sp",
        split_axis=0,
        concat_axis=1,
        tiled=True,
    )
    mix_rows = apply_table("wk,lkc->lwc", cas_width, returned).reshape(row_count, chan_part)
    offset = lax.axis_index("ch") * chan_part
    local_pool = jnp.mean(jnp.take(embed_table, prompt_ids, axis=1).astype(jnp.float32), axis=1)
    pooled_all = lax.all_gather(local_pool, ("sp", "ch"), axis=0, tiled=True)
    pooled = lax.dynamic_slice_in_dim(pooled_all, offset, chan_part)
    channel = offset + jnp.arange(chan_part, dtype=jnp.int32)
    modulation = 1.0 + pooled + step_embedding(noise_step, channel, C)
    mixed_rows = (mix_rows * jax.nn.silu(gate_rows) * modulation[None, :]).astype(jnp.bfloat16)
    half_rows = row_count // lax.axis_size("ch")
    own_rows = lax.dynamic_slice_in_dim(full_out, offset, chan_part, 0)
    summed = lax.psum_scatter(
        jnp.dot(mixed_rows, own_rows, preferred_element_type=jnp.float32).astype(jnp.bfloat16),
        "ch",
        scatter_dimension=0,
        tiled=True,
    ).astype(jnp.float32)
    residual = lax.dynamic_slice_in_dim(latents, lax.axis_index("ch") * half_rows, half_rows, 0)
    return (residual.astype(jnp.float32) + summed).astype(jnp.bfloat16)


def solution(mesh):
    placed = (
        P(("grp", "sp"), None),
        P(None, None, "sp", "ch"),
        P("sp", "ch"),
        P("sp", "ch"),
        P("sp", None),
        P(("sp", "ch"), None),
        P("grp"),
        P("grp"),
    )
    return jax.shard_map(
        local, mesh=mesh, in_specs=placed, out_specs=P(("grp", "sp", "ch"), None), check_vma=False
    )
```

profile of v0, /device:TPU:0, one launch (start us, length us, event | category | flops | bytes accessed | tf_op | source)
XLA Modules:
  0.0 687.1 jit_solution(4367004813713135409)
XLA Ops:
  6.5 0.0 all-gather.4.cloned.1.call-start
  6.5 0.7 all-gather.4.cloned.1.call-update
  7.3 61.9 %all-gather.4.cloned.1.call-done = bf16[1024,1024]{1,0:T(8,128)(2,1)} async-done(((bf16[32,1024]{1,0:T(8,128)(2,1)}), bf16[1024,1024]{1,0:T(8,128)(2,1)}) %all-gather.4.cloned.1.call-update) | async-done | bytes 2097168 | tf_op jit(solution)/shard_map/all_gather | solution.py:38
  69.1 12.8 %convolution_convert_fusion = bf16[4096,1024]{1,0:T(8,128)(2,1)S(1)} fusion(bf16[4096,1024]{1,0:T(8,128)(2,1)} %param.8, bf16[1024,1024]{1,0:T(8,128)(2,1)} %all-gather.4.cloned.1.call-done), kind=kOutput, calls=%fused_computation.18 | convolution fusion | flops 8594128896 | bytes 18874368 | tf_op jit(solution)/shard_map/dot_general | solution.py:42
  82.0 5.1 convert_bitcast_fusion.2
  87.1 12.4 %copy.18 = bf16[32,128,1024]{2,0,1:T(8,128)(2,1)} copy(bf16[32,128,1024]{1,2,0:T(8,128)(2,1)} %convert_bitcast_fusion.2) | data formatting | bytes 16777216 | tf_op jit(solution)/shard_map/convert_element_type | solution.py:50
  99.5 187.2 %all_to_all.33 = bf16[32,128,1024]{2,0,1:T(8,128)(2,1)} all-to-all(bf16[32,128,1024]{2,0,1:T(8,128)(2,1)} %copy.18), channel_id=1, replica_groups=mesh['grp'=1,'sp'=32,'ch'=1] {'sp'}, dimensions={1} | all-to-all | bytes 16777216 | tf_op jit(solution)/shard_map/all_to_all | solution.py:51
  286.7 8.6 %copy.19 = bf16[32,32,4,1024]{3,1,0,2:T(8,128)(2,1)} copy(bf16[32,32,4,1024]{3,1,2,0:T(8,128)(2,1)} %bitcast.48) | data formatting | bytes 16777216 | tf_op jit(solution)/shard_map/all_to_all | solution.py:51
  295.3 9.1 %convert_bitcast_fusion.1 = bf16[16,64,4,1024]{3,1,2,0:T(8,128)(2,1)} fusion(bf16[16,64,4,1024]{3,1,0,2:T(8,128)(2,1)} %bitcast.49), kind=kOutput, calls=%fused_computation.16 | convolution fusion | flops 541134848 | bytes 16777216 | tf_op jit(solution)/shard_map/ah,thkc->takc/dot_general | solution.py:31
  304.4 26.9 %fusion.15 = bf16[16,64,4,1024]{3,0,2,1:T(8,128)(2,1)} fusion(bf16[16,64,4,1024]{3,2,1,0:T(4,128)(2,1)} %param.9, bf16[16,64,4,1024]{3,1,2,0:T(8,128)(2,1)} %convert_bitcast_fusion.1), kind=kOutput, calls=%fused_computation.19 | convolution fusion | flops 293609984 | bytes 25165824 | tf_op jit(solution)/shard_map/ts,sakc->takc/dot_general | solution.py:31
  331.3 17.6 %convert_bitcast_fusion = bf16[16,64,4,1024]{3,1,2,0:T(8,128)(2,1)} fusion(bf16[16,64,4,1024]{3,0,2,1:T(8,128)(2,1)} %fusion.15), kind=kOutput, calls=%fused_computation.14 | convolution fusion | flops 541134848 | bytes 16777216 | tf_op jit(solution)/shard_map/ha,takc->thkc/dot_general | solution.py:31
  348.9 8.6 %copy.24 = bf16[16,64,4,1024]{3,1,0,2:T(8,128)(2,1)} copy(bf16[16,64,4,1024]{3,1,2,0:T(8,128)(2,1)} %convert_bitcast_fusion) | data formatting | bytes 16777216 | tf_op jit(solution)/shard_map/convert_element_type | solution.py:58
  357.5 12.3 %copy.25 = bf16[1024,4,1024]{2,1,0:T(4,128)(2,1)} copy(bf16[1024,4,1024]{2,0,1:T(8,128)(2,1)} %bitcast.50) | data formatting | bytes 16777216 | tf_op jit(solution)/shard_map/reshape | solution.py:60
  369.8 0.0 copy-start
  369.8 3.8 all-to-all-start.1
  373.6 0.0 copy-start.1
  373.6 0.0 all-gather.6.cloned.1.call-start
  373.7 0.7 all-gather.6.cloned.1.call-update
  374.4 0.0 all-gather.8.cloned.1.call-start
  374.4 0.7 all-gather.8.cloned.1.call-update
  375.1 0.0 copy-done
  375.2 5.9 copy.28
  381.7 0.0 copy-done.1
  381.8 5.2 gather_fusion
  387.0 0.1 convert_reduce_fusion
  387.1 0.1 multiply_dynamic-update-slice_fusion
  387.2 210.4 %all-reduce = f32[1024]{0:T(1024)S(1)} all-reduce(f32[1024]{0:T(1024)S(1)} %multiply_dynamic-update-slice_fusion), channel_id=1, replica_groups=mesh['grp'=1,'sp'=32,'ch'=1] {'sp','ch'}, use_global_device_ids=true, to_apply=%add | all-reduce | flops 1024 | bytes 8192
  597.6 0.0 all-to-all-done.1
  597.6 9.6 %copy.26 = bf16[1024,4,1024]{2,0,1:T(8,128)(2,1)} copy(bf16[1024,4,1024]{2,1,0:T(4,128)(2,1)} %all-to-all-done.1) | data formatting | bytes 16777216 | tf_op jit(solution)/shard_map/all_to_all | solution.py:59
  607.3 12.2 %copy.27 = bf16[32,32,4,1024]{3,2,1,0:T(4,128)(2,1)} copy(bf16[32,32,4,1024]{3,0,1,2:T(8,128)(2,1)} %bitcast.51) | data formatting | bytes 16777216 | tf_op jit(solution)/shard_map/all_to_all | solution.py:59
  619.5 12.5 %all_to_all.30 = bf16[32,128,1024]{2,1,0:T(8,128)(2,1)} reshape(bf16[32,32,4,1024]{3,2,1,0:T(4,128)(2,1)} %copy.27) | data formatting | bytes 16777216 | tf_op jit(solution)/shard_map/all_to_all | solution.py:59
  631.9 11.7 %fusion.32 = f32[32,1024,128]{1,2,0:T(8,128)} fusion(bf16[32,128,1024]{2,1,0:T(8,128)(2,1)} %all_to_all.30), kind=kOutput, calls=%fused_computation.41 | convolution fusion | flops 1074020352 | bytes 25165824 | tf_op jit(solution)/shard_map/wk,lkc->lwc/dot_general | solution.py:31
  643.6 0.0 all-gather.6.cloned.1.call-done
  643.6 20.4 %fusion.1 = bf16[4096,1024]{1,0:T(8,128)(2,1)} fusion(f32[32,1024,128]{1,2,0:T(8,128)} %fusion.32, f32[1024]{0:T(1024)S(1)} %select_add_fusion, bf16[4096,1024]{1,0:T(8,128)(2,1)} %param.8, bf16[1024,1024]{1,0:T(8,128)(2,1)} %all-gather.6.cloned.1.call-done), kind=kOutput, calls=%fused_computation.3 | convolution fusion | flops 8619294720 | bytes 35655680 | tf_op jit(solution)/shard_map/dot_general | solution.py:45
  664.0 0.0 all-gather.8.cloned.1.call-done
  664.0 16.1 %add_convert_fusion = bf16[4096,1024]{1,0:T(8,128)(2,1)} fusion(bf16[4096,1024]{1,0:T(8,128)(2,1)} %param.8, bf16[4096,1024]{1,0:T(8,128)(2,1)} %fusion.1, bf16[1024,1024]{1,0:T(8,128)(2,1)} %all-gather.8.cloned.1.call-done), kind=kOutput, calls=%fused_computation.4 | convolution fusion | flops 8610906112 | bytes 27262976 | tf_op jit(solution)/shard_map/dot_general | solution.py:77
  (5 shorter events, 0.1 us)
Async XLA Ops:
  6.5 62.6 %all-gather.4.cloned.1.call-start = ((), (), s32[]{:S(2)}) async-start(), calls=%async_computation.2 | async-start | bytes 2162688 | tf_op jit(solution)/shard_map/all_gather | solution.py:38
  369.8 5.3 copy-start
  369.8 227.8 %all-to-all-start.1 = ((bf16[1024,4,1024]{2,1,0:T(4,128)(2,1)}), bf16[1024,4,1024]{2,1,0:T(4,128)(2,1)}, u32[]{:S(2)}, u32[]{:S(2)}) async-start(bf16[1024,4,1024]{2,1,0:T(4,128)(2,1)} %copy.25), calls=%async_computation.1 | async-start | bytes 16777216 | tf_op jit(solution)/shard_map/all_to_all | solution.py:59
  373.6 8.1 %copy-start.1 = (s32[256]{0:T(256)S(1)}, s32[256]{0:T(256)}, u32[]{:S(2)}) copy-start(s32[256]{0:T(256)} %param.14) | copy-start | bytes 3076
  373.6 270.0 %all-gather.6.cloned.1.call-start = ((), (), s32[]{:S(2)}) async-start(), calls=%async_computation.3 | async-start | bytes 2162688 | tf_op jit(solution)/shard_map/all_gather | solution.py:39
  374.4 289.6 %all-gather.8.cloned.1.call-start = ((), (), s32[]{:S(2)}) async-start(), calls=%async_computation.4 | async-start | bytes 2162688 | tf_op jit(solution)/shard_map/all_gather | solution.py:40
Sparse Core Ops, SparseCore 0:
  10.2 58.9 all-gather.3
  377.3 96.9 all-gather.5
  477.2 78.9 all-gather.7
where the time goes:
time: 695 us; the launch traced here: 687 us
  blocking collectives  398 us (57%)
  matrix products  120 us (17%)
  local copies, waits for them, and re-layouts  87.4 us (13%)
  waiting for transfers between devices  64 us (9%)
  between operations  14.3 us (2%)
    unnamed x1, blocking collectives  210 us
    all_to_all x1, blocking collectives, local(): lax.all_to_all(width_spec, 'sp', split_axis=1, concat_axis=0, tiled=True)  187 us
    dot_general x5, matrix products, apply_table(): return jnp.einsum(form, table, operand, preferred_element_type=jnp.float32)  70.4 us
    all_gather x1, waiting for transfers between devices, local(): lax.all_gather(w_value, 'sp', axis=0, tiled=True)  61.9 us
    all_to_all x3, local copies, waits for them, and re-layouts, local(): lax.all_to_all(height_back.reshape(TT * HH, band_count, chan_part), 'sp',...  34.3 us
    dot_general x1, matrix products, local(): gate_rows = jnp.dot(latents, full_gate, preferred_element_type=jnp.float32)  20.4 us
    dot_general x1, matrix products, local(): jnp.dot(mixed_rows, own_rows, preferred_element_type=jnp.float32)  16.1 us
  transfers between devices with their start and end apart: 4, of which 1 were waited for; matrix products, arithmetic and copies ran while one was open for 10% of the time, Pallas kernels for 0%

commit v1 on v0

--- a/solution.py
+++ b/solution.py
@@ -1,8 +1,12 @@
+import functools
 import math
 
 import jax
 import jax.numpy as jnp
+import numpy as np
 from jax import lax
+from jax.experimental import pallas as pl
+from jax.experimental.pallas import tpu as pltpu
 from jax.sharding import PartitionSpec as P
 
 TT = 16
@@ -31,7 +35,7 @@
     return jnp.einsum(form, table, operand, preferred_element_type=jnp.float32)
 
 
-def local(latents, spectrum, w_value, w_gate, w_out, embed_table, prompt_ids, noise_step):
+def local_split_channels(latents, spectrum, w_value, w_gate, w_out, embed_table, prompt_ids, noise_step):
     row_count = latents.shape[0]
     chan_part = w_value.shape[1]
     full_value, full_gate, full_out = (
@@ -82,6 +86,222 @@
     residual = lax.dynamic_slice_in_dim(latents, lax.axis_index("ch") * half_rows, half_rows, 0)
     return (residual.astype(jnp.float32) + summed).astype(jnp.bfloat16)
 
+SUB = 8
+MIB = 1 << 20
+
+
+def cas_host(length):
+    position = np.arange(length)
+    phase_angle = (position[:, None] * position[None, :] % length).astype(np.float32) * np.float32(
+        2.0 * math.pi / length
+    )
+    table = (np.cos(phase_angle) + np.sin(phase_angle)) / np.float32(math.sqrt(length))
+    return table.astype(jnp.bfloat16).astype(np.float32)
+
+
+def width_table(devices, band_count, bands):
+    frequency = (np.arange(devices)[:, None] * band_count + np.asarray(bands)[None, :]).reshape(-1)
+    rows = cas_host(WW)[frequency]
+    return np.einsum("fw,lm->flmw", rows, np.eye(SUB, dtype=np.float32)).reshape(
+        len(frequency) * SUB, SUB * WW
+    ).astype(jnp.bfloat16)
+
+
+def plane_table():
+    return np.kron(cas_host(TT), cas_host(HH)).astype(jnp.bfloat16)
+
+
+def dot32(left, right, contract=(1, 0)):
+    return lax.dot_general(
+        left, right, (((contract[0],), (contract[1],)), ((), ())), preferred_element_type=jnp.float32
+    )
+
+
+def forward_body(table_ref, rows_ref, out_ref):
+    spec = dot32(table_ref[...], rows_ref[...])
+    out_ref[...] = spec.reshape(out_ref.shape).astype(jnp.bfloat16)
+
+
+def width_forward(table, latents, devices, bands):
+    rows, chans = latents.shape
+    group = SUB * WW
+    lines = rows // WW
+    return pl.pallas_call(
+        forward_body,
+        name="width_forward",
+        grid=(rows // group,),
+        in_specs=[
+            pl.BlockSpec(table.shape, lambda g: (0, 0)),
+            pl.BlockSpec((group, chans), lambda g: (g, 0)),
+        ],
+        out_specs=pl.BlockSpec((devices, bands, SUB, chans), lambda g: (0, 0, g, 0)),
+        out_shape=jax.ShapeDtypeStruct((devices, bands, lines, chans), jnp.bfloat16),
+        compiler_params=pltpu.CompilerParams(
+            dimension_semantics=("arbitrary",), vmem_limit_bytes=58 * MIB
+        ),
+        cost_estimate=pl.CostEstimate(
+            flops=2 * rows * chans * table.shape[0],
+            bytes_accessed=4 * rows * chans,
+            transcendentals=0,
+        ),
+    )(table, latents)
+
+
+def plane_body(table_ref, value_ref, spectrum_ref, pencil_ref, out_ref, first_ref, second_ref):
+    cells, chans = first_ref.shape
+    step = min(cells, 256)
+    pencil = pencil_ref[...].reshape(cells, chans)
+    for at in range(0, cells, step):
+        part = pl.ds(at, step)
+        first_ref[part, :] = dot32(table_ref[part, :], pencil).astype(jnp.bfloat16)
+    for at in range(0, cells, step):
+        part = pl.ds(at, step)
+        full = dot32(first_ref[part, :], value_ref[...])
+        gain = spectrum_ref[0, part, :].astype(jnp.float32)
+        second_ref[part, :] = (full * gain).astype(jnp.bfloat16)
+    devices, _, lines, _ = out_ref.shape
+    per = step // lines
+    for at in range(0, cells, step):
+        back = dot32(table_ref[pl.ds(at, step), :], second_ref[...]).astype(jnp.bfloat16)
+        out_ref[pl.ds(at // lines, per), :, :, :] = back.reshape(per, 1, lines, chans)
+
+
+def plane_filter(table, w_value, spectrum, pencil, first_band):
+    devices, bands, lines, chans = pencil.shape
+    cells = devices * lines
+    block = pl.BlockSpec((devices, 1, lines, chans), lambda j: (0, j, 0, 0))
+    return pl.pallas_call(
+        plane_body,
+        name="plane_filter",
+        grid=(bands,),
+        in_specs=[
+            pl.BlockSpec(table.shape, lambda j: (0, 0)),
+            pl.BlockSpec(w_value.shape, lambda j: (0, 0)),
+            pl.BlockSpec((1, cells, chans), lambda j: (first_band + j, 0, 0)),
+            block,
+        ],
+        out_specs=block,
+        out_shape=jax.ShapeDtypeStruct(pencil.shape, jnp.bfloat16),
+        scratch_shapes=[pltpu.VMEM((cells, chans), jnp.bfloat16)] * 2,
+        compiler_params=pltpu.CompilerParams(
+            dimension_semantics=("arbitrary",), vmem_limit_bytes=58 * MIB
+        ),
+        cost_estimate=pl.CostEstimate(
+            flops=2 * bands * cells * chans * (2 * cells + chans),
+            bytes_accessed=6 * bands * cells * chans,
+            transcendentals=0,
+        ),
+    )(table, w_value, spectrum, pencil)
+
+
+def finish_body(*refs):
+    parts = (len(refs) - 4) // 2
+    tables, spectra = refs[:parts], refs[parts : 2 * parts]
+    gate_ref, latents_ref, w_out_ref, out_ref = refs[2 * parts :]
+    chans = out_ref.shape[1]
+    mix = None
+    for table_ref, spec_ref in zip(tables, spectra):
+        spec = spec_ref[...].astype(jnp.float32).reshape(table_ref.shape[0], chans)
+        term = dot32(table_ref[...], spec.astype(jnp.bfloat16), (0, 0))
+        mix = term if mix is None else mix + term
+    mixed = (mix * gate_ref[...].astype(jnp.float32)).astype(jnp.bfloat16)
+    out = latents_ref[...].astype(jnp.float32) + dot32(mixed, w_out_ref[...])
+    out_ref[...] = out.astype(jnp.bfloat16)
+
+
+def finish(tables, spectra, gate, latents, w_out):
+    rows, chans = latents.shape
+    group = SUB * WW
+    by_group = pl.BlockSpec((group, chans), lambda g: (g, 0))
+    whole = lambda g: (0, 0)
+    return pl.pallas_call(
+        finish_body,
+        name="finish",
+        grid=(rows // group,),
+        in_specs=[pl.BlockSpec(table.shape, whole) for table in tables]
+        + [
+            pl.BlockSpec(spec.shape[:2] + (SUB, chans), lambda g: (0, 0, g, 0))
+            for spec in spectra
+        ]
+        + [by_group, by_group, pl.BlockSpec(w_out.shape, whole)],
+        out_specs=by_group,
+        out_shape=jax.ShapeDtypeStruct((rows, chans), jnp.bfloat16),
+        compiler_params=pltpu.CompilerParams(
+            dimension_semantics=("arbitrary",), vmem_limit_bytes=58 * MIB
+        ),
+        cost_estimate=pl.CostEstimate(
+            flops=2 * rows * chans * (group + chans),
+            bytes_accessed=8 * rows * chans,
+            transcendentals=0,
+        ),
+    )(*tables, *spectra, gate, latents, w_out)
+
+
+def gather_blocks(block, axis, devices):
+    own = lax.axis_index(axis)
+    held = block[None]
+    bit = devices // 2
+    order = []
+    while bit:
+        pairs = [(i, i ^ bit) for i in range(devices)]
+        other = lax.ppermute(held, axis, pairs)
+        held = jnp.concatenate([held, other], axis=0)
+        order = order + [slot ^ bit for slot in order] if order else [0, bit]
+        bit //= 2
+    slot_of = np.argsort(np.asarray(order))
+    return held, slot_of, own
+
+
+def in_device_order(held, slot_of, own):
+    devices = held.shape[0]
+    slots = jnp.asarray(slot_of, jnp.int32)[jnp.arange(devices, dtype=jnp.int32) ^ own]
+    return jnp.take(held, slots, axis=0)
+
+
+def local_planes(
+    devices, latents, spectrum, w_value, w_gate, w_out, embed_table, prompt_ids, noise_step
+):
+    row_count, chans = latents.shape
+    band_count = spectrum.shape[2]
+    half = max(band_count // 2, 1)
+    chunks = [tuple(range(at, min(at + half, band_count))) for at in range(0, band_count, half)]
+    tables = [jnp.asarray(width_table(devices, band_count, bands)) for bands in chunks]
+    plane = jnp.asarray(plane_table())
+
+    sent = [width_forward(table, latents, devices, len(b)) for table, b in zip(tables, chunks)]
+    pencils = [
+        lax.all_to_all(part, "sp", split_axis=0, concat_axis=0, tiled=True) for part in sent
+    ]
+
+    weights = jnp.concatenate([w_value, w_gate, w_out], axis=0)
+    held, slot_of, own = gather_blocks(weights, "sp", devices)
+    ordered = in_device_order(held, slot_of, own)
+    per = w_value.shape[0]
+    full_value = ordered[:, :per].reshape(-1, chans)
+    full_gate = ordered[:, per : 2 * per].reshape(-1, chans)
+    full_out = ordered[:, 2 * per :].reshape(-1, chans)
+
+    local_pool = jnp.mean(jnp.take(embed_table, prompt_ids, axis=1).astype(jnp.float32), axis=1)
+    pool_held, pool_slot, _ = gather_blocks(local_pool, "sp", devices)
+    pooled = in_device_order(pool_held, pool_slot, own).reshape(-1)
+    channel = jnp.arange(chans, dtype=jnp.int32)
+    modulation = 1.0 + pooled + step_embedding(noise_step, channel, chans)
+    gate_rows = jnp.dot(latents, full_gate, preferred_element_type=jnp.float32)
+    gate = (jax.nn.silu(gate_rows) * modulation[None, :]).astype(jnp.bfloat16)
+
+    gain = spectrum.transpose(2, 0, 1, 3).reshape(band_count, TT * HH, chans)
+    returned = [
+        lax.all_to_all(
+            plane_filter(plane, full_value, gain, pencil, bands[0]),
+            "sp",
+            split_axis=0,
+            concat_axis=0,
+            tiled=True,
+        )
+        for pencil, bands in zip(pencils, chunks)
+    ]
+    return finish(tables, returned, gate, latents, full_out)
+
 
 def solution(mesh):
     placed = (
@@ -94,6 +314,10 @@
         P("grp"),
         P("grp"),
     )
+    devices = mesh.shape["sp"]
+    lines = TT * HH // devices
+    planes = mesh.shape["ch"] == 1 and devices & (devices - 1) == 0 and lines % SUB == 0
+    local = functools.partial(local_planes, devices) if planes else local_split_channels
     return jax.shard_map(
         local, mesh=mesh, in_specs=placed, out_specs=P(("grp", "sp", "ch"), None), check_vma=False
     )

time: 695 us -> 522 us (0.75); the launches traced: 687 us -> 521 us
  blocking collectives: 398 us -> 0 us
  waiting for transfers between devices: 64 us -> 338 us
  matrix products: 120 us -> 17.8 us
  Pallas kernels: 0 us -> 78.4 us
  local copies, waits for them, and re-layouts: 87.4 us -> 38.7 us
  starting transfers between devices: 3.9 us -> 43 us
  between operations: 14.3 us -> 0.84 us
    ppermute x0 -> x10, waiting for transfers between devices: none -> 262 us  [gather_blocks(): other = lax.ppermute(held, axis, pairs)]
    unnamed x1 -> x0, blocking collectives: 210 us -> none
    all_to_all x1 -> x0, blocking collectives: 187 us -> none  [local(): lax.all_to_all(width_spec, 'sp', split_axis=1, concat_axis=0, tiled=True)]
    dot_general x8 -> x1, matrix products: 120 us -> 17.8 us  [local_planes(): gate_rows = jnp.dot(latents, full_gate, preferred_element_type=jnp.float32)]
    pallas_call x0 -> x5, Pallas kernels: none -> 78.4 us  [the longest x2 36.6 us: plane_filter(): pl.pallas_call(plane_body, name='plane_filter', grid=(bands,), in_specs=[...]
    all_to_all x1 -> x4, waiting for transfers between devices: 0.01 us -> 75.4 us  [the longest x2 75.4 us: local_planes(): lax.all_to_all(plane_filter(plane, full_value, gain, pencil, bands[0]), '...]
    all_gather x3 -> x0, waiting for transfers between devices: 61.9 us -> none  [the longest x1 61.9 us: local(): lax.all_gather(w_value, 'sp', axis=0, tiled=True)]
    all_to_all x4 -> x0, local copies, waits for them, and re-layouts: 42.9 us -> none  [the longest x3 34.3 us: local(): lax.all_to_all(height_back.reshape(TT * HH, band_count, chan_part), 'sp',...]
  transfers between devices with their start and end apart: 4 -> 14, of which waited for: 1 -> 10; matrix products, arithmetic and copies ran while one was open for 10% -> 12% of each run, Pallas kernels for 0% -> 9%
where the time goes in v1:
time: 522 us; the launch traced here: 521 us
  waiting for transfers between devices  338 us (65%)
  Pallas kernels  78.4 us (15%)
  starting transfers between devices  43 us (8%)
  local copies, waits for them, and re-layouts  38.7 us (7%)
  matrix products  17.8 us (3%)
    ppermute x10, waiting for transfers between devices, gather_blocks(): other = lax.ppermute(held, axis, pairs)  262 us
    all_to_all x2, waiting for transfers between devices, local_planes(): lax.all_to_all(plane_filter(plane, full_value, gain, pencil, bands[0]), '...  75.4 us
    pallas_call x2, Pallas kernels, plane_filter(): pl.pallas_call(plane_body, name='plane_filter', grid=(bands,), in_specs=[...  36.6 us
    pallas_call x1, Pallas kernels, finish(): pl.pallas_call(finish_body, name='finish', grid=(rows // group,), in_spec...  24.3 us
    dot_general x1, matrix products, local_planes(): gate_rows = jnp.dot(latents, full_gate, preferred_element_type=jnp.float32)  17.8 us
    ppermute x10, starting transfers between devices, gather_blocks(): other = lax.ppermute(held, axis, pairs)  17.7 us
    pallas_call x2, Pallas kernels, width_forward(): pl.pallas_call(forward_body, name='width_forward', grid=(rows // group,),...  17.6 us
    all_to_all x2, starting transfers between devices, local_planes(): lax.all_to_all(plane_filter(plane, full_value, gain, pencil, bands[0]), '...  13.7 us
  transfers between devices with their start and end apart: 14, of which 10 were waited for; matrix products, arithmetic and copies ran while one was open for 12% of the time, Pallas kernels for 9%

profile of v1, /device:TPU:0, one launch (start us, length us, event | category | flops | bytes accessed | tf_op | source)
XLA Modules:
  0.0 521.2 jit_solution(14177658802640522904)
XLA Ops:
  0.0 8.7 %width_forward.2 = bf16[32,2,32,1024]{3,2,1,0:T(8,128)(2,1)} custom-call(bf16[512,1024]{1,0:T(8,128)(2,1)} %constant.75.clone.table_ref.refs_0_, bf16[4096,1024]{1,0:T(8,128)(2,1)} %refs_5_.1), custom_call_target="tpu_custom_call" | custom-call | flops 4294967296 | bytes 16777216 | tf_op jit(solution)/shard_map/width_forward/pallas_call | solution.py:129
  8.8 7.5 %all-to-all-start = ((bf16[32,2,32,1024]{3,2,1,0:T(8,128)(2,1)}), bf16[32,2,32,1024]{3,2,1,0:T(8,128)(2,1)}, u32[]{:S(2)}, u32[]{:S(2)}) async-start(bf16[32,2,32,1024]{3,2,1,0:T(8,128)(2,1)} %width_forward.2), calls=%async_computation | async-start | bytes 8388608 | tf_op jit(solution)/shard_map/all_to_all | solution.py:273
  16.3 2.7 collective-permute-start
  18.9 99.3 %collective-permute-done = bf16[1,96,1024]{2,1,0:T(8,128)(2,1)S(1)} collective-permute-done((bf16[1,96,1024]{2,1,0:T(8,128)(2,1)S(1)}, bf16[1,96,1024]{2,1,0:T(8,128)(2,1)S(1)}, u32[]{:S(2)}, u32[]{:S(2)}) %collective-permute-start) | collective-permute-done | bytes 196640 | tf_op jit(solution)/shard_map/ppermute | solution.py:247
  118.3 0.1 collective-permute-start.1
  118.4 10.5 %collective-permute-done.1 = bf16[2,96,1024]{2,1,0:T(8,128)(2,1)S(1)} collective-permute-done((bf16[2,96,1024]{2,1,0:T(8,128)(2,1)S(1)}, bf16[2,96,1024]{2,1,0:T(8,128)(2,1)S(1)}, u32[]{:S(2)}, u32[]{:S(2)}) %collective-permute-start.1) | collective-permute-done | bytes 393248 | tf_op jit(solution)/shard_map/ppermute | solution.py:247
  128.9 0.1 pad_maximum_fusion.1
  129.0 1.5 collective-permute-start.2
  130.5 8.8 %width_forward.3 = bf16[32,2,32,1024]{3,2,1,0:T(8,128)(2,1)} custom-call(bf16[512,1024]{1,0:T(8,128)(2,1)} %constant.76.clone.table_ref.refs_1_, bf16[4096,1024]{1,0:T(8,128)(2,1)} %refs_5_.1), custom_call_target="tpu_custom_call" | custom-call | flops 4294967296 | bytes 16777216 | tf_op jit(solution)/shard_map/width_forward/pallas_call | solution.py:129
  139.3 4.1 all-to-all-start.2
  143.4 15.5 %collective-permute-done.2 = bf16[4,96,1024]{2,1,0:T(8,128)(2,1)S(1)} collective-permute-done((bf16[4,96,1024]{2,1,0:T(8,128)(2,1)S(1)}, bf16[4,96,1024]{2,1,0:T(8,128)(2,1)S(1)}, u32[]{:S(2)}, u32[]{:S(2)}) %collective-permute-start.2) | collective-permute-done | bytes 786464 | tf_op jit(solution)/shard_map/ppermute | solution.py:247
  159.0 0.2 pad_maximum_fusion
  159.1 7.7 %collective-permute-start.3 = (bf16[8,96,1024]{2,1,0:T(8,128)(2,1)S(1)}, bf16[8,96,1024]{2,1,0:T(8,128)(2,1)S(1)}, u32[]{:S(2)}, u32[]{:S(2)}) collective-permute-start(bf16[8,96,1024]{2,1,0:T(8,128)(2,1)S(1)} %pad_maximum_fusion), channel_id=1, source_target_pairs={{0,2},{1,3},{2,0},{3,1},{4,6},{5,7},{6,4},{7,5},{8,10},{9,11},{10,... | collective-permute-start | bytes 4718600 | tf_op jit(solution)/shard_map/ppermute | solution.py:247
  166.8 0.8 constant_dynamic-update-slice_fusion.4
  167.7 0.8 constant_dynamic-update-slice_fusion.3
  168.5 1.0 constant_dynamic-update-slice_fusion.2
  169.5 1.4 constant_dynamic-update-slice_fusion.1
  170.8 48.6 %collective-permute-done.3 = bf16[8,96,1024]{2,1,0:T(8,128)(2,1)S(1)} collective-permute-done((bf16[8,96,1024]{2,1,0:T(8,128)(2,1)S(1)}, bf16[8,96,1024]{2,1,0:T(8,128)(2,1)S(1)}, u32[]{:S(2)}, u32[]{:S(2)}) %collective-permute-start.3) | collective-permute-done | bytes 1572896 | tf_op jit(solution)/shard_map/ppermute | solution.py:247
  219.4 2.1 constant_dynamic-update-slice_fusion
  221.5 9.7 %copy.17 = bf16[4,16,64,1024]{3,2,1,0:T(8,128)(2,1)} copy(bf16[4,16,64,1024]{3,0,2,1:T(4,128)(2,1)} %bitcast.37) | data formatting | bytes 16777216 | tf_op jit(solution)/shard_map/transpose | solution.py:292
  231.2 0.7 gather_fusion
  232.0 2.0 constant_dynamic-update-slice_fusion.5
  234.0 6.4 %gather_fusion.1 = bf16[32,96,1024]{2,1,0:T(8,128)(2,1)} fusion(bf16[32,96,1024]{2,1,0:T(8,128)(2,1)} %constant_dynamic-update-slice_fusion.5, s32[1024]{0:T(1024)S(1)} %pad_clamp_fusion.1), kind=kCustom, calls=%fused_computation.1 | custom fusion | bytes 12583040 | tf_op jit(solution)/shard_map/jit(_take)/gather | solution.py:258
  240.4 3.4 broadcast_select_fusion
  243.8 2.8 fusion.11
  246.6 18.3 %plane_filter.2 = bf16[32,2,32,1024]{3,2,1,0:T(8,128)(2,1)} custom-call(bf16[1024,1024]{1,0:T(8,128)(2,1)} %constant.77.clone.table_ref, bf16[1024,1024]{1,0:T(8,128)(2,1)} %bitcast.42, bf16[4,1024,1024]{2,1,0:T(8,128)(2,1)} %bitcast.38, bf16[32,2,32,1024]{3,2,1,0:T(8,128)(2,1)} %all-to-all-done.pencil_ref), custom_call_target="tpu_custom_call" | custom-call | flops 12884901888 | bytes 12582912 | tf_op jit(solution)/shard_map/plane_filter/pallas_call | solution.py:173
  264.9 9.7 %all-to-all-start.1 = ((bf16[32,2,32,1024]{3,2,1,0:T(8,128)(2,1)}), bf16[32,2,32,1024]{3,2,1,0:T(8,128)(2,1)}, u32[]{:S(2)}, u32[]{:S(2)}) async-start(bf16[32,2,32,1024]{3,2,1,0:T(8,128)(2,1)} %plane_filter.2), calls=%async_computation.1 | async-start | bytes 8388608 | tf_op jit(solution)/shard_map/all_to_all | solution.py:294
  274.6 18.3 %plane_filter.3 = bf16[32,2,32,1024]{3,2,1,0:T(8,128)(2,1)} custom-call(bf16[1024,1024]{1,0:T(8,128)(2,1)} %constant.77.clone.table_ref, bf16[1024,1024]{1,0:T(8,128)(2,1)} %bitcast.43, bf16[4,1024,1024]{2,1,0:T(8,128)(2,1)} %bitcast.39, bf16[32,2,32,1024]{3,2,1,0:T(8,128)(2,1)} %all-to-all-done.2.pencil_ref), custom_call_target="tpu_custom_call" | custom-call | flops 12884901888 | bytes 12582912 | tf_op jit(solution)/shard_map/plane_filter/pallas_call | solution.py:173
  292.9 75.4 %all-to-all-done.1.refs_2_ = bf16[32,2,32,1024]{3,2,1,0:T(8,128)(2,1)} async-done(((bf16[32,2,32,1024]{3,2,1,0:T(8,128)(2,1)}), bf16[32,2,32,1024]{3,2,1,0:T(8,128)(2,1)}, u32[]{:S(2)}, u32[]{:S(2)}) %all-to-all-start.1) | async-done | bytes 4194336 | tf_op jit(solution)/shard_map/all_to_all | solution.py:294
  368.3 4.0 all-to-all-start.3
  372.4 5.9 %copy.19 = bf16[32,32768]{0,1:T(8,128)(2,1)} copy(bf16[32,32768]{1,0:T(8,128)(2,1)S(1)} %copy-done.1) | data formatting | bytes 4194304 | tf_op args[5]
  378.3 5.2 gather_fusion.2
  383.5 0.1 convert_reduce_fusion
  383.6 2.7 collective-permute-start.5
  386.3 79.8 %collective-permute-done.5 = f32[1,32]{1,0:T(1,128)S(1)} collective-permute-done((f32[1,32]{1,0:T(1,128)S(1)}, f32[1,32]{1,0:T(1,128)S(1)}, u32[]{:S(2)}, u32[]{:S(2)}) %collective-permute-start.5) | collective-permute-done | bytes 160 | tf_op jit(solution)/shard_map/ppermute | solution.py:247
  466.1 0.1 collective-permute-start.6
  466.2 3.6 collective-permute-done.6
  469.7 1.5 collective-permute-start.7
  471.2 2.2 collective-permute-done.7
  473.4 1.5 collective-permute-start.8
  474.9 2.2 collective-permute-done.8
  477.1 0.1 collective-permute-start.9
  477.8 0.5 collective-permute-done.9
  478.3 0.6 gather_fusion.3
  478.9 0.1 select_add_fusion
  479.0 0.1 add.92
  479.1 17.8 %fusion.4.refs_4_ = bf16[4096,1024]{1,0:T(8,128)(2,1)} fusion(f32[1024]{0:T(1024)S(1)} %select_add_fusion.1, bf16[4096,1024]{1,0:T(8,128)(2,1)} %refs_5_.1, bf16[1024,1024]{1,0:T(8,128)(2,1)} %bitcast.41), kind=kOutput, calls=%fused_computation.10 | convolution fusion | flops 8615100416 | bytes 18878464 | tf_op jit(solution)/shard_map/dot_general | solution.py:289
  496.9 24.3 %finish.1 = bf16[4096,1024]{1,0:T(8,128)(2,1)} custom-call(bf16[512,1024]{1,0:T(8,128)(2,1)} %constant.75.clone.table_ref.refs_0_, bf16[512,1024]{1,0:T(8,128)(2,1)} %constant.76.clone.table_ref.refs_1_, bf16[32,2,32,1024]{3,2,1,0:T(8,128)(2,1)} %all-to-all-done.1.refs_2_, bf16[32,2,32,1024]{3,2,1,0:T(8,128)(2,1)} %all-to-all-done.3.refs_3_, ...), custom_call_target="tpu_custom_call" | custom-call | flops 17179869184 | bytes 33554432 | tf_op jit(solution)/shard_map/finish/pallas_call | solution.py:217
  (33 shorter events, 0.3 us)
Async XLA Ops:
  8.7 7.5 %copy-start.2 = (bf16[32,1024]{1,0:T(8,128)(2,1)S(1)}, bf16[32,1024]{1,0:T(8,128)(2,1)}, u32[]{:S(2)}) copy-start(bf16[32,1024]{1,0:T(8,128)(2,1)} %param.17) | copy-start | bytes 196612
  8.7 7.5 %copy-start.3 = (bf16[32,1024]{1,0:T(8,128)(2,1)S(1)}, bf16[32,1024]{1,0:T(8,128)(2,1)}, u32[]{:S(2)}) copy-start(bf16[32,1024]{1,0:T(8,128)(2,1)} %param.16) | copy-start | bytes 196612
  8.7 7.5 %copy-start.4 = (bf16[32,1024]{1,0:T(8,128)(2,1)S(1)}, bf16[32,1024]{1,0:T(8,128)(2,1)}, u32[]{:S(2)}) copy-start(bf16[32,1024]{1,0:T(8,128)(2,1)} %param.15) | copy-start | bytes 196612
  8.8 130.6 %all-to-all-start = ((bf16[32,2,32,1024]{3,2,1,0:T(8,128)(2,1)}), bf16[32,2,32,1024]{3,2,1,0:T(8,128)(2,1)}, u32[]{:S(2)}, u32[]{:S(2)}) async-start(bf16[32,2,32,1024]{3,2,1,0:T(8,128)(2,1)} %width_forward.2), calls=%async_computation | async-start | bytes 8388608 | tf_op jit(solution)/shard_map/all_to_all | solution.py:273
  16.3 102.0 %collective-permute-start = (bf16[1,96,1024]{2,1,0:T(8,128)(2,1)S(1)}, bf16[1,96,1024]{2,1,0:T(8,128)(2,1)S(1)}, u32[]{:S(2)}, u32[]{:S(2)}) collective-permute-start(bf16[1,96,1024]{2,1,0:T(8,128)(2,1)S(1)} %maximum_bitcast_fusion), channel_id=1, source_target_pairs={{0,16},{1,17},{2,18},{3,19},{4,20},{5,21},{6,22},{7,23},{8,24},{9,... | collective-permute-start | bytes 589832 | tf_op jit(solution)/shard_map/ppermute | solution.py:247
  118.3 10.6 %collective-permute-start.1 = (bf16[2,96,1024]{2,1,0:T(8,128)(2,1)S(1)}, bf16[2,96,1024]{2,1,0:T(8,128)(2,1)S(1)}, u32[]{:S(2)}, u32[]{:S(2)}) collective-permute-start(bf16[2,96,1024]{2,1,0:T(8,128)(2,1)S(1)} %pad_maximum_fusion.2), channel_id=1, source_target_pairs={{0,8},{1,9},{2,10},{3,11},{4,12},{5,13},{6,14},{7,15},{8,0},{9,1},... | collective-permute-start | bytes 1179656 | tf_op jit(solution)/shard_map/ppermute | solution.py:247
  129.0 30.0 %collective-permute-start.2 = (bf16[4,96,1024]{2,1,0:T(8,128)(2,1)S(1)}, bf16[4,96,1024]{2,1,0:T(8,128)(2,1)S(1)}, u32[]{:S(2)}, u32[]{:S(2)}) collective-permute-start(bf16[4,96,1024]{2,1,0:T(8,128)(2,1)S(1)} %pad_maximum_fusion.1), channel_id=1, source_target_pairs={{0,4},{1,5},{2,6},{3,7},{4,0},{5,1},{6,2},{7,3},{8,12},{9,13},{10,... | collective-permute-start | bytes 2359304 | tf_op jit(solution)/shard_map/ppermute | solution.py:247
  139.3 125.6 %all-to-all-start.2 = ((bf16[32,2,32,1024]{3,2,1,0:T(8,128)(2,1)}), bf16[32,2,32,1024]{3,2,1,0:T(8,128)(2,1)}, u32[]{:S(2)}, u32[]{:S(2)}) async-start(bf16[32,2,32,1024]{3,2,1,0:T(8,128)(2,1)} %width_forward.3), calls=%async_computation.2 | async-start | bytes 8388608 | tf_op jit(solution)/shard_map/all_to_all | solution.py:273
  159.1 60.3 %collective-permute-start.3 = (bf16[8,96,1024]{2,1,0:T(8,128)(2,1)S(1)}, bf16[8,96,1024]{2,1,0:T(8,128)(2,1)S(1)}, u32[]{:S(2)}, u32[]{:S(2)}) collective-permute-start(bf16[8,96,1024]{2,1,0:T(8,128)(2,1)S(1)} %pad_maximum_fusion), channel_id=1, source_target_pairs={{0,2},{1,3},{2,0},{3,1},{4,6},{5,7},{6,4},{7,5},{8,10},{9,11},{10,... | collective-permute-start | bytes 4718600 | tf_op jit(solution)/shard_map/ppermute | solution.py:247
  221.5 10.4 %collective-permute-start.4 = (bf16[16,96,1024]{2,1,0:T(8,128)(2,1)}, bf16[16,96,1024]{2,1,0:T(8,128)(2,1)S(1)}, u32[]{:S(2)}, u32[]{:S(2)}) collective-permute-start(bf16[16,96,1024]{2,1,0:T(8,128)(2,1)} %get-tuple-element.8), channel_id=1, source_target_pairs={{0,1},{1,0},{2,3},{3,2},{4,5},{5,4},{6,7},{7,6},{8,9},{9,8},{10,11... | collective-permute-start | bytes 9437192 | tf_op jit(solution)/shard_map/ppermute | solution.py:247
  221.5 9.7 %copy-start.5 = (s32[256]{0:T(256)S(1)}, s32[256]{0:T(256)}, u32[]{:S(2)}) copy-start(s32[256]{0:T(256)} %param.19) | copy-start | bytes 3076
  221.5 9.7 %copy-start = (s32[32]{0:T(128)S(1)}, s32[32]{0:T(128)}, u32[]{:S(2)}) copy-start(s32[32]{0:T(128)} %constant.78.clone) | copy-start | bytes 388
  264.9 103.4 %all-to-all-start.1 = ((bf16[32,2,32,1024]{3,2,1,0:T(8,128)(2,1)}), bf16[32,2,32,1024]{3,2,1,0:T(8,128)(2,1)}, u32[]{:S(2)}, u32[]{:S(2)}) async-start(bf16[32,2,32,1024]{3,2,1,0:T(8,128)(2,1)} %plane_filter.2), calls=%async_computation.1 | async-start | bytes 8388608 | tf_op jit(solution)/shard_map/all_to_all | solution.py:294
  292.9 79.4 %copy-start.1 = (bf16[32,32768]{1,0:T(8,128)(2,1)S(1)}, bf16[32,32768]{1,0:T(8,128)(2,1)}, u32[]{:S(2)}) copy-start(bf16[32,32768]{1,0:T(8,128)(2,1)} %param.18) | copy-start | bytes 6291460
  368.3 128.6 %all-to-all-start.3 = ((bf16[32,2,32,1024]{3,2,1,0:T(8,128)(2,1)}), bf16[32,2,32,1024]{3,2,1,0:T(8,128)(2,1)}, u32[]{:S(2)}, u32[]{:S(2)}) async-start(bf16[32,2,32,1024]{3,2,1,0:T(8,128)(2,1)} %plane_filter.3), calls=%async_computation.3 | async-start | bytes 8388608 | tf_op jit(solution)/shard_map/all_to_all | solution.py:294
  383.6 82.5 %collective-permute-start.5 = (f32[1,32]{1,0:T(1,128)S(1)}, f32[1,32]{1,0:T(1,128)S(1)}, u32[]{:S(2)}, u32[]{:S(2)}) collective-permute-start(f32[1,32]{1,0:T(1,128)S(1)} %multiply_bitcast_fusion), channel_id=1, source_target_pairs={{0,16},{1,17},{2,18},{3,19},{4,20},{5,21},{6,22},{7,23},{8,24},{9,... | collective-permute-start | bytes 392 | tf_op jit(solution)/shard_map/ppermute | solution.py:247
  466.1 3.6 collective-permute-start.6
  469.7 3.7 collective-permute-start.7
  473.4 3.7 collective-permute-start.8
  477.1 1.2 collective-permute-start.9

commit v2 on v1

--- a/solution.py
+++ b/solution.py
@@ -8,6 +8,7 @@
 from jax.experimental import pallas as pl
 from jax.experimental.pallas import tpu as pltpu
 from jax.sharding import PartitionSpec as P
+
 
 TT = 16
 HH = 64
@@ -86,6 +87,7 @@
     residual = lax.dynamic_slice_in_dim(latents, lax.axis_index("ch") * half_rows, half_rows, 0)
     return (residual.astype(jnp.float32) + summed).astype(jnp.bfloat16)
 
+
 SUB = 8
 MIB = 1 << 20
 
@@ -120,6 +122,12 @@
 def forward_body(table_ref, rows_ref, out_ref):
     spec = dot32(table_ref[...], rows_ref[...])
     out_ref[...] = spec.reshape(out_ref.shape).astype(jnp.bfloat16)
+
+
+def kernel_params(axes):
+    return pltpu.CompilerParams(
+        dimension_semantics=("arbitrary",) * axes, vmem_limit_bytes=58 * MIB
+    )
 
 
 def width_forward(table, latents, devices, bands):
@@ -136,9 +144,7 @@
         ],
         out_specs=pl.BlockSpec((devices, bands, SUB, chans), lambda g: (0, 0, g, 0)),
         out_shape=jax.ShapeDtypeStruct((devices, bands, lines, chans), jnp.bfloat16),
-        compiler_params=pltpu.CompilerParams(
-            dimension_semantics=("arbitrary",), vmem_limit_bytes=58 * MIB
-        ),
+        compiler_params=kernel_params(1),
         cost_estimate=pl.CostEstimate(
             flops=2 * rows * chans * table.shape[0],
             bytes_accessed=4 * rows * chans,
@@ -147,9 +153,11 @@
     )(table, latents)
 
 
-def plane_body(table_ref, value_ref, spectrum_ref, pencil_ref, out_ref, first_ref, second_ref):
+def plane_body(table_ref, value_ref, spectrum_ref, pencil_ref, *rest):
+    out_refs, (first_ref, second_ref) = rest[:-2], rest[-2:]
     cells, chans = first_ref.shape
     step = min(cells, 256)
+    lines = pencil_ref.shape[2]
     pencil = pencil_ref[...].reshape(cells, chans)
     for at in range(0, cells, step):
         part = pl.ds(at, step)
@@ -159,17 +167,21 @@
         full = dot32(first_ref[part, :], value_ref[...])
         gain = spectrum_ref[0, part, :].astype(jnp.float32)
         second_ref[part, :] = (full * gain).astype(jnp.bfloat16)
-    devices, _, lines, _ = out_ref.shape
     per = step // lines
     for at in range(0, cells, step):
-        back = dot32(table_ref[pl.ds(at, step), :], second_ref[...]).astype(jnp.bfloat16)
-        out_ref[pl.ds(at // lines, per), :, :, :] = back.reshape(per, 1, lines, chans)
-
-
-def plane_filter(table, w_value, spectrum, pencil, first_band):
+        back = dot32(table_ref[pl.ds(at, step), :], second_ref[...])
+        back = back.reshape(per, lines, chans).astype(jnp.bfloat16)
+        line = 0
+        for out_ref in out_refs:
+            count = out_ref.shape[2]
+            out_ref[pl.ds(at // lines, per), 0] = back[:, line : line + count]
+            line += count
+
+
+def plane_filter(table, w_value, spectrum, pencil, first_band, splits):
     devices, bands, lines, chans = pencil.shape
     cells = devices * lines
-    block = pl.BlockSpec((devices, 1, lines, chans), lambda j: (0, j, 0, 0))
+    block = lambda count: pl.BlockSpec((devices, 1, count, chans), lambda j: (0, j, 0, 0))
     return pl.pallas_call(
         plane_body,
         name="plane_filter",
@@ -178,14 +190,14 @@
             pl.BlockSpec(table.shape, lambda j: (0, 0)),
             pl.BlockSpec(w_value.shape, lambda j: (0, 0)),
             pl.BlockSpec((1, cells, chans), lambda j: (first_band + j, 0, 0)),
-            block,
+            block(lines),
         ],
-        out_specs=block,
-        out_shape=jax.ShapeDtypeStruct(pencil.shape, jnp.bfloat16),
+        out_specs=[block(count) for count in splits],
+        out_shape=[
+            jax.ShapeDtypeStruct((devices, bands, count, chans), jnp.bfloat16) for count in splits
+        ],
         scratch_shapes=[pltpu.VMEM((cells, chans), jnp.bfloat16)] * 2,
-        compiler_params=pltpu.CompilerParams(
-            dimension_semantics=("arbitrary",), vmem_limit_bytes=58 * MIB
-        ),
+        compiler_params=kernel_params(1),
         cost_estimate=pl.CostEstimate(
             flops=2 * bands * cells * chans * (2 * cells + chans),
             bytes_accessed=6 * bands * cells * chans,
@@ -194,113 +206,153 @@
     )(table, w_value, spectrum, pencil)
 
 
-def finish_body(*refs):
-    parts = (len(refs) - 4) // 2
+def finish_body(parts, *refs):
     tables, spectra = refs[:parts], refs[parts : 2 * parts]
-    gate_ref, latents_ref, w_out_ref, out_ref = refs[2 * parts :]
-    chans = out_ref.shape[1]
+    gate_ref, latents_ref, w_out_ref = refs[2 * parts : 2 * parts + 3]
+    out_ref, spec_refs = refs[-1 - parts], refs[-parts:]
+
+    @pl.when(pl.program_id(1) == 0)
+    def _():
+        for source, held in zip(spectra, spec_refs):
+            wide = source[...].astype(jnp.float32).reshape(held.shape)
+            held[...] = wide.astype(jnp.bfloat16)
+
     mix = None
-    for table_ref, spec_ref in zip(tables, spectra):
-        spec = spec_ref[...].astype(jnp.float32).reshape(table_ref.shape[0], chans)
-        term = dot32(table_ref[...], spec.astype(jnp.bfloat16), (0, 0))
+    for table_ref, held in zip(tables, spec_refs):
+        term = dot32(table_ref[...], held[...], (0, 0))
         mix = term if mix is None else mix + term
     mixed = (mix * gate_ref[...].astype(jnp.float32)).astype(jnp.bfloat16)
     out = latents_ref[...].astype(jnp.float32) + dot32(mixed, w_out_ref[...])
     out_ref[...] = out.astype(jnp.bfloat16)
 
 
-def finish(tables, spectra, gate, latents, w_out):
+def finish(tables, spectra, starts, gate, latents, w_out, groups, done=None):
     rows, chans = latents.shape
     group = SUB * WW
-    by_group = pl.BlockSpec((group, chans), lambda g: (g, 0))
-    whole = lambda g: (0, 0)
+    first, count = groups
+    pieces = 4
+    piece = group // pieces
+    by_piece = pl.BlockSpec((piece, chans), lambda g, s: ((first + g) * pieces + s, 0))
+    spec_block = lambda spec, start: pl.BlockSpec(
+        spec.shape[:2] + (SUB, chans), lambda g, s: (0, 0, first + g - start, 0)
+    )
+    inputs = [*tables, *spectra, gate, latents, w_out] + ([] if done is None else [done])
     return pl.pallas_call(
-        finish_body,
+        functools.partial(finish_body, len(tables)),
         name="finish",
-        grid=(rows // group,),
-        in_specs=[pl.BlockSpec(table.shape, whole) for table in tables]
-        + [
-            pl.BlockSpec(spec.shape[:2] + (SUB, chans), lambda g: (0, 0, g, 0))
-            for spec in spectra
+        grid=(count, pieces),
+        in_specs=[
+            pl.BlockSpec((table.shape[0], piece), lambda g, s: (0, s)) for table in tables
         ]
-        + [by_group, by_group, pl.BlockSpec(w_out.shape, whole)],
-        out_specs=by_group,
+        + [spec_block(spec, start) for spec, start in zip(spectra, starts)]
+        + [by_piece, by_piece, pl.BlockSpec(w_out.shape, lambda g, s: (0, 0))]
+        + ([] if done is None else [pl.BlockSpec(memory_space=pl.ANY)]),
+        out_specs=by_piece,
         out_shape=jax.ShapeDtypeStruct((rows, chans), jnp.bfloat16),
-        compiler_params=pltpu.CompilerParams(
-            dimension_semantics=("arbitrary",), vmem_limit_bytes=58 * MIB
-        ),
+        scratch_shapes=[pltpu.VMEM((table.shape[0], chans), jnp.bfloat16) for table in tables],
+        input_output_aliases={} if done is None else {len(inputs) - 1: 0},
+        compiler_params=kernel_params(2),
         cost_estimate=pl.CostEstimate(
-            flops=2 * rows * chans * (group + chans),
-            bytes_accessed=8 * rows * chans,
+            flops=2 * count * group * chans * (group + chans),
+            bytes_accessed=8 * count * group * chans,
             transcendentals=0,
         ),
-    )(*tables, *spectra, gate, latents, w_out)
-
-
-def gather_blocks(block, axis, devices):
-    own = lax.axis_index(axis)
+    )(*inputs)
+
+
+def exchange(tensor):
+    return lax.all_to_all(tensor, "sp", split_axis=0, concat_axis=0, tiled=True)
+
+
+def spread(held, bits, devices):
+    deltas = [0]
+    for bit in bits:
+        deltas = deltas + [delta ^ bit for delta in deltas]
+    blocks = [held]
+    for delta in deltas[1:]:
+        pairs = [(i, i ^ delta) for i in range(devices)]
+        blocks.append(lax.ppermute(held, "sp", pairs))
+    return blocks, deltas
+
+
+def gather_blocks(block, stages, devices):
+    order = [0]
     held = block[None]
-    bit = devices // 2
-    order = []
-    while bit:
-        pairs = [(i, i ^ bit) for i in range(devices)]
-        other = lax.ppermute(held, axis, pairs)
-        held = jnp.concatenate([held, other], axis=0)
-        order = order + [slot ^ bit for slot in order] if order else [0, bit]
-        bit //= 2
-    slot_of = np.argsort(np.asarray(order))
-    return held, slot_of, own
-
-
-def in_device_order(held, slot_of, own):
-    devices = held.shape[0]
-    slots = jnp.asarray(slot_of, jnp.int32)[jnp.arange(devices, dtype=jnp.int32) ^ own]
+    for bits in stages:
+        blocks, deltas = spread(held, bits, devices)
+        held = jnp.concatenate(blocks, axis=0)
+        order = [slot ^ delta for delta in deltas for slot in order]
+    slot_of = jnp.asarray(np.argsort(np.asarray(order)), jnp.int32)
+    own = lax.axis_index("sp")
+    slots = slot_of[jnp.arange(devices, dtype=jnp.int32) ^ own]
     return jnp.take(held, slots, axis=0)
 
 
-def local_planes(
-    devices, latents, spectrum, w_value, w_gate, w_out, embed_table, prompt_ids, noise_step
-):
+def gather_stages(devices):
+    bits = [1 << at for at in range(devices.bit_length() - 1)]
+    return [stage for stage in (bits[3:], bits[1:3], bits[:1]) if stage]
+
+
+def chunks_of(band_count):
+    return [(0,)] + ([tuple(range(1, band_count))] if band_count > 1 else [])
+
+
+def splits_of(lines):
+    return [lines - SUB, SUB] if lines > SUB else [lines]
+
+
+def local_planes(devices, *args):
+    return planes(devices, *args)
+
+
+def planes(devices, latents, spectrum, w_value, w_gate, w_out, embed_table, prompt_ids, noise_step):
     row_count, chans = latents.shape
     band_count = spectrum.shape[2]
-    half = max(band_count // 2, 1)
-    chunks = [tuple(range(at, min(at + half, band_count))) for at in range(0, band_count, half)]
+    lines = row_count // WW
+    chunks = chunks_of(band_count)
+    splits = splits_of(lines)
+    stages = gather_stages(devices)
     tables = [jnp.asarray(width_table(devices, band_count, bands)) for bands in chunks]
     plane = jnp.asarray(plane_table())
-
-    sent = [width_forward(table, latents, devices, len(b)) for table, b in zip(tables, chunks)]
-    pencils = [
-        lax.all_to_all(part, "sp", split_axis=0, concat_axis=0, tiled=True) for part in sent
-    ]
-
-    weights = jnp.concatenate([w_value, w_gate, w_out], axis=0)
-    held, slot_of, own = gather_blocks(weights, "sp", devices)
-    ordered = in_device_order(held, slot_of, own)
     per = w_value.shape[0]
-    full_value = ordered[:, :per].reshape(-1, chans)
-    full_gate = ordered[:, per : 2 * per].reshape(-1, chans)
-    full_out = ordered[:, 2 * per :].reshape(-1, chans)
-
-    local_pool = jnp.mean(jnp.take(embed_table, prompt_ids, axis=1).astype(jnp.float32), axis=1)
-    pool_held, pool_slot, _ = gather_blocks(local_pool, "sp", devices)
-    pooled = in_device_order(pool_held, pool_slot, own).reshape(-1)
-    channel = jnp.arange(chans, dtype=jnp.int32)
+
+    pencils = []
+    for table, bands in zip(tables, chunks):
+        part = width_forward(table, latents, devices, len(bands))
+        pencils.append(exchange(part))
+
+    both = gather_blocks(jnp.concatenate([w_value, w_gate], axis=0), stages, devices)
+    full_value = both[:, :per].reshape(-1, chans)
+    full_gate = both[:, per:].reshape(-1, chans)
+
+    taken = jnp.take(embed_table, prompt_ids, axis=1).astype(jnp.float32)
+    pooled = jnp.mean(taken, axis=1)
+    channel = lax.axis_index("sp") * per + jnp.arange(per, dtype=jnp.int32)
     modulation = 1.0 + pooled + step_embedding(noise_step, channel, chans)
+    scaled = (w_out.astype(jnp.float32) * modulation[:, None]).astype(jnp.bfloat16)
+    full_out = gather_blocks(scaled, stages, devices).reshape(-1, chans)
+
+    gain = spectrum.transpose(2, 0, 1, 3).reshape(band_count, TT * HH, chans)
+
+    returned = []
+    for at, (pencil, bands) in enumerate(zip(pencils, chunks)):
+        last = at == len(chunks) - 1
+        parts = plane_filter(plane, full_value, gain, pencil, bands[0], splits if last else [lines])
+        returned.append([exchange(part) for part in parts])
+
     gate_rows = jnp.dot(latents, full_gate, preferred_element_type=jnp.float32)
-    gate = (jax.nn.silu(gate_rows) * modulation[None, :]).astype(jnp.bfloat16)
-
-    gain = spectrum.transpose(2, 0, 1, 3).reshape(band_count, TT * HH, chans)
-    returned = [
-        lax.all_to_all(
-            plane_filter(plane, full_value, gain, pencil, bands[0]),
-            "sp",
-            split_axis=0,
-            concat_axis=0,
-            tiled=True,
+    gate = jax.nn.silu(gate_rows).astype(jnp.bfloat16)
+
+    done, line = None, 0
+    for piece, count in enumerate(splits):
+        spectra = [back[min(piece, len(back) - 1)] for back in returned]
+        starts = [0 if len(back) == 1 else line // SUB for back in returned]
+        done = finish(
+            tables, spectra, starts, gate, latents, full_out,
+            (line // SUB, count // SUB), done,
         )
-        for pencil, bands in zip(pencils, chunks)
-    ]
-    return finish(tables, returned, gate, latents, full_out)
+        line += count
+    return done
 
 
 def solution(mesh):
@@ -316,8 +368,8 @@
     )
     devices = mesh.shape["sp"]
     lines = TT * HH // devices
-    planes = mesh.shape["ch"] == 1 and devices & (devices - 1) == 0 and lines % SUB == 0
-    local = functools.partial(local_planes, devices) if planes else local_split_channels
+    whole_channels = mesh.shape["ch"] == 1 and devices & (devices - 1) == 0 and lines % SUB == 0
+    local = functools.partial(local_planes, devices) if whole_channels else local_split_channels
     return jax.shard_map(
         local, mesh=mesh, in_specs=placed, out_specs=P(("grp", "sp", "ch"), None), check_vma=False
     )

time: 522 us -> 526 us (level)
  waiting for transfers between devices: 338 us -> 324 us
  local copies, waits for them, and re-layouts: 38.7 us -> 49.6 us
  Pallas kernels: 78.4 us -> 85.7 us
    all_to_all x4 -> x5, waiting for transfers between devices: 75.4 us -> 61.5 us  [exchange(): return lax.all_to_all(tensor, 'sp', split_axis=0, concat_axis=0, tiled=True)]
    unnamed x16 -> x28, local copies, waits for them, and re-layouts: 9.13 us -> 19.8 us
    pallas_call x1 -> x2, Pallas kernels: 24.3 us -> 31.7 us  [finish(): pl.pallas_call(functools.partial(finish_body, len(tables)), name='finish'...]
    ppermute x10 -> x14, starting transfers between devices: 17.7 us -> 16 us  [spread(): blocks.append(lax.ppermute(held, 'sp', pairs))]
    all_to_all x4 -> x5, starting transfers between devices: 25.3 us -> 25.7 us  [exchange(): return lax.all_to_all(tensor, 'sp', split_axis=0, concat_axis=0, tiled=True)]
    ppermute x10 -> x14, waiting for transfers between devices: 262 us -> 262 us  [spread(): blocks.append(lax.ppermute(held, 'sp', pairs))]
  transfers between devices with their start and end apart: 14 -> 19, of which waited for: 10 -> 11; matrix products, arithmetic and copies ran while one was open for 12% -> 13% of each run, Pallas kernels for 9% -> 13%
where the time goes in v2:
time: 526 us; the launch traced here: 525 us
  waiting for transfers between devices  324 us (62%)
  Pallas kernels  85.7 us (16%)
  local copies, waits for them, and re-layouts  49.6 us (9%)
  starting transfers between devices  41.7 us (8%)
  matrix products  17.3 us (3%)
  other arithmetic  5.55 us (1%)
    ppermute x14, waiting for transfers between devices, spread(): blocks.append(lax.ppermute(held, 'sp', pairs))  262 us
    all_to_all x5, waiting for transfers between devices, exchange(): return lax.all_to_all(tensor, 'sp', split_axis=0, concat_axis=0, tiled=True)  61.5 us
    pallas_call x2, Pallas kernels, plane_filter(): pl.pallas_call(plane_body, name='plane_filter', grid=(bands,), in_specs=[...  36.5 us
    pallas_call x2, Pallas kernels, finish(): pl.pallas_call(functools.partial(finish_body, len(tables)), name='finish'...  31.7 us
    all_to_all x5, starting transfers between devices, exchange(): return lax.all_to_all(tensor, 'sp', split_axis=0, concat_axis=0, tiled=True)  25.7 us
    unnamed x28, local copies, waits for them, and re-layouts  19.8 us
    pallas_call x2, Pallas kernels, width_forward(): pl.pallas_call(forward_body, name='width_forward', grid=(rows // group,),...  17.5 us
    dot_general x1, matrix products, planes(): gate_rows = jnp.dot(latents, full_gate, preferred_element_type=jnp.float32)  17.3 us
  transfers between devices with their start and end apart: 19, of which 11 were waited for; matrix products, arithmetic and copies ran while one was open for 13% of the time, Pallas kernels for 13%

profile of v2, /device:TPU:0, one launch (start us, length us, event | category | flops | bytes accessed | tf_op | source)
XLA Modules:
  0.0 524.5 jit_solution(14820993579622625079)
XLA Ops:
  0.0 6.6 %width_forward.2 = bf16[32,1,32,1024]{3,2,1,0:T(8,128)(2,1)} custom-call(bf16[256,1024]{1,0:T(8,128)(2,1)} %constant.75.clone.table_ref.refs_0_, bf16[4096,1024]{1,0:T(8,128)(2,1)} %refs_5_.3), custom_call_target="tpu_custom_call" | custom-call | flops 2147483648 | bytes 16777216 | tf_op jit(solution)/shard_map/width_forward/pallas_call | solution.py:137
  6.6 7.3 %all-to-all-start = ((bf16[32,1,32,1024]{3,2,1,0:T(8,128)(2,1)}), bf16[32,1,32,1024]{3,2,1,0:T(8,128)(2,1)S(1)}, u32[]{:S(2)}, u32[]{:S(2)}) async-start(bf16[32,1,32,1024]{3,2,1,0:T(8,128)(2,1)} %width_forward.2), calls=%async_computation | async-start | bytes 4194304 | tf_op jit(solution)/shard_map/all_to_all | solution.py:264
  13.9 10.9 %width_forward.3 = bf16[32,3,32,1024]{3,2,1,0:T(8,128)(2,1)} custom-call(bf16[768,1024]{1,0:T(8,128)(2,1)} %constant.76.clone.table_ref.refs_1_, bf16[4096,1024]{1,0:T(8,128)(2,1)} %refs_5_.3), custom_call_target="tpu_custom_call" | custom-call | flops 6442450944 | bytes 16777216 | tf_op jit(solution)/shard_map/width_forward/pallas_call | solution.py:137
  24.8 37.9 %all-to-all-done.pencil_ref = bf16[32,1,32,1024]{3,2,1,0:T(8,128)(2,1)S(1)} async-done(((bf16[32,1,32,1024]{3,2,1,0:T(8,128)(2,1)}), bf16[32,1,32,1024]{3,2,1,0:T(8,128)(2,1)S(1)}, u32[]{:S(2)}, u32[]{:S(2)}) %all-to-all-start) | async-done | bytes 2097184 | tf_op jit(solution)/shard_map/all_to_all | solution.py:264
  62.7 1.4 copy-done.3
  64.0 4.2 all-to-all-start.2
  68.3 1.8 collective-permute-start
  70.1 2.4 collective-permute-start.1
  72.7 102.0 %collective-permute-done = bf16[1,64,1024]{2,1,0:T(8,128)(2,1)S(1)} collective-permute-done((bf16[1,64,1024]{2,1,0:T(8,128)(2,1)S(1)}, bf16[1,64,1024]{2,1,0:T(8,128)(2,1)S(1)}, u32[]{:S(2)}, u32[]{:S(2)}) %collective-permute-start) | collective-permute-done | bytes 131104 | tf_op jit(solution)/shard_map/ppermute | solution.py:274
  174.7 42.2 %collective-permute-done.1 = bf16[1,64,1024]{2,1,0:T(8,128)(2,1)S(1)} collective-permute-done((bf16[1,64,1024]{2,1,0:T(8,128)(2,1)S(1)}, bf16[1,64,1024]{2,1,0:T(8,128)(2,1)S(1)}, u32[]{:S(2)}, u32[]{:S(2)}) %collective-permute-start.1) | collective-permute-done | bytes 131104 | tf_op jit(solution)/shard_map/ppermute | solution.py:274
  217.3 2.0 collective-permute-start.4
  219.3 0.8 constant_dynamic-update-slice_fusion.6
  220.1 1.2 collective-permute-start.5
  223.5 8.3 %collective-permute-done.3 = bf16[4,64,1024]{2,1,0:T(8,128)(2,1)S(1)} collective-permute-done((bf16[4,64,1024]{2,1,0:T(8,128)(2,1)S(1)}, bf16[4,64,1024]{2,1,0:T(8,128)(2,1)S(1)}, u32[]{:S(2)}, u32[]{:S(2)}) %collective-permute-start.3) | collective-permute-done | bytes 524320 | tf_op jit(solution)/shard_map/ppermute | solution.py:274
  231.8 1.2 constant_dynamic-update-slice_fusion.2
  233.0 8.3 %collective-permute-done.4 = bf16[4,64,1024]{2,1,0:T(8,128)(2,1)S(1)} collective-permute-done((bf16[4,64,1024]{2,1,0:T(8,128)(2,1)S(1)}, bf16[4,64,1024]{2,1,0:T(8,128)(2,1)S(1)}, u32[]{:S(2)}, u32[]{:S(2)}) %collective-permute-start.4) | collective-permute-done | bytes 524320 | tf_op jit(solution)/shard_map/ppermute | solution.py:274
  241.3 1.1 constant_dynamic-update-slice_fusion.1
  242.4 1.1 constant_dynamic-update-slice_fusion
  243.6 9.7 %copy.18 = bf16[4,16,64,1024]{3,2,1,0:T(8,128)(2,1)} copy(bf16[4,16,64,1024]{3,0,2,1:T(4,128)(2,1)} %bitcast.37) | data formatting | bytes 16777216 | tf_op jit(solution)/shard_map/transpose | solution.py:335
  254.0 1.5 constant_dynamic-update-slice_fusion.7
  255.5 5.0 gather_fusion.1
  260.5 2.6 broadcast_select_fusion
  263.1 2.5 fusion.13
  265.6 11.5 %plane_filter.2 = bf16[32,1,32,1024]{3,2,1,0:T(8,128)(2,1)} custom-call(bf16[1024,1024]{1,0:T(8,128)(2,1)} %constant.77.clone.table_ref, bf16[1024,1024]{1,0:T(8,128)(2,1)} %bitcast.41, bf16[4,1024,1024]{2,1,0:T(8,128)(2,1)} %bitcast.38, bf16[32,1,32,1024]{3,2,1,0:T(8,128)(2,1)} %copy-done.3), custom_call_target="tpu_custom_call" | custom-call | flops 6442450944 | bytes 6291456 | tf_op jit(solution)/shard_map/plane_filter/pallas_call | solution.py:185
  277.1 5.7 %all-to-all-start.1 = ((bf16[32,1,32,1024]{3,2,1,0:T(8,128)(2,1)}), bf16[32,1,32,1024]{3,2,1,0:T(8,128)(2,1)S(1)}, u32[]{:S(2)}, u32[]{:S(2)}) async-start(bf16[32,1,32,1024]{3,2,1,0:T(8,128)(2,1)} %plane_filter.2), calls=%async_computation.1 | async-start | bytes 4194304 | tf_op jit(solution)/shard_map/all_to_all | solution.py:264
  282.8 25.0 %plane_filter.3 = (bf16[32,3,24,1024]{3,2,1,0:T(8,128)(2,1)}, bf16[32,3,8,1024]{3,2,1,0:T(8,128)(2,1)}) custom-call(bf16[1024,1024]{1,0:T(8,128)(2,1)} %constant.77.clone.table_ref, bf16[1024,1024]{1,0:T(8,128)(2,1)} %bitcast.42, bf16[4,1024,1024]{2,1,0:T(8,128)(2,1)} %bitcast.39, bf16[32,3,32,1024]{3,2,1,0:T(8,128)(2,1)} %all-to-all-done.2.pencil_ref), custom_call_target="tpu_custom_call" | custom-call | flops 19327352832 | bytes 18874368 | tf_op jit(solution)/shard_map/plane_filter/pallas_call | solution.py:185
  307.8 23.7 %all-to-all-done.1.refs_2_ = bf16[32,1,32,1024]{3,2,1,0:T(8,128)(2,1)S(1)} async-done(((bf16[32,1,32,1024]{3,2,1,0:T(8,128)(2,1)}), bf16[32,1,32,1024]{3,2,1,0:T(8,128)(2,1)S(1)}, u32[]{:S(2)}, u32[]{:S(2)}) %all-to-all-start.1) | async-done | bytes 2097184 | tf_op jit(solution)/shard_map/all_to_all | solution.py:264
  331.5 1.3 copy-done.1
  332.8 4.1 all-to-all-start.4
  336.9 7.4 %copy.20 = bf16[32,32768]{0,1:T(8,128)(2,1)} copy(bf16[32,32768]{1,0:T(8,128)(2,1)} %param.18) | data formatting | bytes 4194304 | tf_op args[5]
  344.9 5.2 gather_fusion.2
  350.4 1.8 collective-permute-start.7
  352.2 2.4 collective-permute-start.8
  355.5 61.0 %collective-permute-done.7 = bf16[1,32,1024]{2,1,0:T(8,128)(2,1)S(1)} collective-permute-done((bf16[1,32,1024]{2,1,0:T(8,128)(2,1)S(1)}, bf16[1,32,1024]{2,1,0:T(8,128)(2,1)S(1)}, u32[]{:S(2)}, u32[]{:S(2)}) %collective-permute-start.7) | collective-permute-done | bytes 65568 | tf_op jit(solution)/shard_map/ppermute | solution.py:274
  416.5 30.2 %collective-permute-done.8 = bf16[1,32,1024]{2,1,0:T(8,128)(2,1)S(1)} collective-permute-done((bf16[1,32,1024]{2,1,0:T(8,128)(2,1)S(1)}, bf16[1,32,1024]{2,1,0:T(8,128)(2,1)S(1)}, u32[]{:S(2)}, u32[]{:S(2)}) %collective-permute-start.8) | collective-permute-done | bytes 65568 | tf_op jit(solution)/shard_map/ppermute | solution.py:274
  446.7 1.3 collective-permute-start.10
  448.0 1.8 collective-permute-start.11
  452.2 3.8 collective-permute-done.10
  456.7 4.0 collective-permute-done.11
  462.3 2.5 collective-permute-done.13
  464.8 1.1 constant_dynamic-update-slice_fusion.22
  465.9 2.3 gather_fusion.3
  468.1 1.7 bitcast_select_fusion.refs_6_
  469.9 4.4 all-to-all-start.3
  474.3 17.3 %fusion.3.refs_4_ = bf16[4096,1024]{1,0:T(8,128)(2,1)} fusion(bf16[4096,1024]{1,0:T(8,128)(2,1)} %refs_5_.3, bf16[1024,1024]{1,0:T(8,128)(2,1)} %bitcast.40), kind=kOutput, calls=%fused_computation.9 | convolution fusion | flops 8610906112 | bytes 18874368 | tf_op jit(solution)/shard_map/dot_general | solution.py:343
  491.6 22.3 %finish.2.refs_7_ = bf16[4096,1024]{1,0:T(8,128)(2,1)} custom-call(bf16[256,1024]{1,0:T(8,128)(2,1)} %constant.75.clone.table_ref.refs_0_, bf16[768,1024]{1,0:T(8,128)(2,1)} %constant.76.clone.table_ref.refs_1_, bf16[32,1,32,1024]{3,2,1,0:T(8,128)(2,1)} %copy-done.1, bf16[32,3,24,1024]{3,2,1,0:T(8,128)(2,1)} %all-to-all-done.4.refs_3_, ...), custom_call_target="tpu_custom_call" | custom-call | flops 12884901888 | bytes 25165824 | tf_op jit(solution)/shard_map/finish/pallas_call | solution.py:240
  513.9 1.2 copy-done.2
  515.1 9.4 %finish.3 = bf16[4096,1024]{1,0:T(8,128)(2,1)} custom-call(bf16[256,1024]{1,0:T(8,128)(2,1)} %constant.75.clone.table_ref.refs_0_, bf16[768,1024]{1,0:T(8,128)(2,1)} %constant.76.clone.table_ref.refs_1_, bf16[32,1,32,1024]{3,2,1,0:T(8,128)(2,1)} %copy-done.1, bf16[32,3,8,1024]{3,2,1,0:T(8,128)(2,1)} %copy-done.2, ...), custom_call_target="tpu_custom_call", output_to_operand_aliasing={{}: (7, {})} | custom-call | flops 4294967296 | bytes 8388608 | tf_op jit(solution)/shard_map/finish/pallas_call | solution.py:240
  (53 shorter events, 9.6 us)
Async XLA Ops:
  6.6 56.1 %all-to-all-start = ((bf16[32,1,32,1024]{3,2,1,0:T(8,128)(2,1)}), bf16[32,1,32,1024]{3,2,1,0:T(8,128)(2,1)S(1)}, u32[]{:S(2)}, u32[]{:S(2)}) async-start(bf16[32,1,32,1024]{3,2,1,0:T(8,128)(2,1)} %width_forward.2), calls=%async_computation | async-start | bytes 4194304 | tf_op jit(solution)/shard_map/all_to_all | solution.py:264
  24.8 43.5 %copy-start.4 = (bf16[32,1024]{1,0:T(8,128)(2,1)S(1)}, bf16[32,1024]{1,0:T(8,128)(2,1)}, u32[]{:S(2)}) copy-start(bf16[32,1024]{1,0:T(8,128)(2,1)} %param.16) | copy-start | bytes 196612
  24.8 43.5 %copy-start.5 = (bf16[32,1024]{1,0:T(8,128)(2,1)S(1)}, bf16[32,1024]{1,0:T(8,128)(2,1)}, u32[]{:S(2)}) copy-start(bf16[32,1024]{1,0:T(8,128)(2,1)} %param.15) | copy-start | bytes 196612
  62.7 1.4 copy-start.3
  64.0 213.0 %all-to-all-start.2 = ((bf16[32,3,32,1024]{3,2,1,0:T(8,128)(2,1)}), bf16[32,3,32,1024]{3,2,1,0:T(8,128)(2,1)}, u32[]{:S(2)}, u32[]{:S(2)}) async-start(bf16[32,3,32,1024]{3,2,1,0:T(8,128)(2,1)} %width_forward.3), calls=%async_computation.2 | async-start | bytes 12582912 | tf_op jit(solution)/shard_map/all_to_all | solution.py:264
  68.3 106.4 %collective-permute-start = (bf16[1,64,1024]{2,1,0:T(8,128)(2,1)S(1)}, bf16[1,64,1024]{2,1,0:T(8,128)(2,1)S(1)}, u32[]{:S(2)}, u32[]{:S(2)}) collective-permute-start(bf16[1,64,1024]{2,1,0:T(8,128)(2,1)S(1)} %maximum_bitcast_fusion), channel_id=1, source_target_pairs={{0,8},{1,9},{2,10},{3,11},{4,12},{5,13},{6,14},{7,15},{8,0},{9,1},... | collective-permute-start | bytes 393224 | tf_op jit(solution)/shard_map/ppermute | solution.py:274
  70.1 146.8 %collective-permute-start.1 = (bf16[1,64,1024]{2,1,0:T(8,128)(2,1)S(1)}, bf16[1,64,1024]{2,1,0:T(8,128)(2,1)S(1)}, u32[]{:S(2)}, u32[]{:S(2)}) collective-permute-start(bf16[1,64,1024]{2,1,0:T(8,128)(2,1)S(1)} %maximum_bitcast_fusion), channel_id=1, source_target_pairs={{0,16},{1,17},{2,18},{3,19},{4,20},{5,21},{6,22},{7,23},{8,24},{9,... | collective-permute-start | bytes 393224 | tf_op jit(solution)/shard_map/ppermute | solution.py:274
  72.5 144.4 %collective-permute-start.2 = (bf16[1,64,1024]{2,1,0:T(8,128)(2,1)S(1)}, bf16[1,64,1024]{2,1,0:T(8,128)(2,1)S(1)}, u32[]{:S(2)}, u32[]{:S(2)}) collective-permute-start(bf16[1,64,1024]{2,1,0:T(8,128)(2,1)S(1)} %maximum_bitcast_fusion), channel_id=1, source_target_pairs={{0,24},{1,25},{2,26},{3,27},{4,28},{5,29},{6,30},{7,31},{8,16},{9,... | collective-permute-start | bytes 393224 | tf_op jit(solution)/shard_map/ppermute | solution.py:274
  217.0 14.9 %collective-permute-start.3 = (bf16[4,64,1024]{2,1,0:T(8,128)(2,1)S(1)}, bf16[4,64,1024]{2,1,0:T(8,128)(2,1)S(1)}, u32[]{:S(2)}, u32[]{:S(2)}) collective-permute-start(bf16[4,64,1024]{2,1,0:T(8,128)(2,1)S(1)} %pad_maximum_fusion), channel_id=1, source_target_pairs={{0,2},{1,3},{2,0},{3,1},{4,6},{5,7},{6,4},{7,5},{8,10},{9,11},{10,... | collective-permute-start | bytes 1572872 | tf_op jit(solution)/shard_map/ppermute | solution.py:274
  217.3 24.0 %collective-permute-start.4 = (bf16[4,64,1024]{2,1,0:T(8,128)(2,1)S(1)}, bf16[4,64,1024]{2,1,0:T(8,128)(2,1)S(1)}, u32[]{:S(2)}, u32[]{:S(2)}) collective-permute-start(bf16[4,64,1024]{2,1,0:T(8,128)(2,1)S(1)} %pad_maximum_fusion), channel_id=1, source_target_pairs={{0,4},{1,5},{2,6},{3,7},{4,0},{5,1},{6,2},{7,3},{8,12},{9,13},{10,... | collective-permute-start | bytes 1572872 | tf_op jit(solution)/shard_map/ppermute | solution.py:274
  220.1 22.4 %collective-permute-start.5 = (bf16[4,64,1024]{2,1,0:T(8,128)(2,1)S(1)}, bf16[4,64,1024]{2,1,0:T(8,128)(2,1)S(1)}, u32[]{:S(2)}, u32[]{:S(2)}) collective-permute-start(bf16[4,64,1024]{2,1,0:T(8,128)(2,1)S(1)} %pad_maximum_fusion), channel_id=1, source_target_pairs={{0,6},{1,7},{2,4},{3,5},{4,2},{5,3},{6,0},{7,1},{8,14},{9,15},{10,... | collective-permute-start | bytes 1572872 | tf_op jit(solution)/shard_map/ppermute | solution.py:274
  243.5 10.4 %collective-permute-start.6 = (bf16[16,64,1024]{2,1,0:T(8,128)(2,1)}, bf16[16,64,1024]{2,1,0:T(8,128)(2,1)S(1)}, u32[]{:S(2)}, u32[]{:S(2)}) collective-permute-start(bf16[16,64,1024]{2,1,0:T(8,128)(2,1)} %get-tuple-element.13), channel_id=1, source_target_pairs={{0,1},{1,0},{2,3},{3,2},{4,5},{5,4},{6,7},{7,6},{8,9},{9,8},{10,11... | collective-permute-start | bytes 6291464 | tf_op jit(solution)/shard_map/ppermute | solution.py:274
  243.6 9.7 %copy-start.7 = (s32[256]{0:T(256)S(1)}, s32[256]{0:T(256)}, u32[]{:S(2)}) copy-start(s32[256]{0:T(256)} %param.19) | copy-start | bytes 3076
  243.6 9.7 %copy-start = (s32[32]{0:T(128)S(1)}, s32[32]{0:T(128)}, u32[]{:S(2)}) copy-start(s32[32]{0:T(128)} %constant.78.clone) | copy-start | bytes 388
  277.1 54.4 %all-to-all-start.1 = ((bf16[32,1,32,1024]{3,2,1,0:T(8,128)(2,1)}), bf16[32,1,32,1024]{3,2,1,0:T(8,128)(2,1)S(1)}, u32[]{:S(2)}, u32[]{:S(2)}) async-start(bf16[32,1,32,1024]{3,2,1,0:T(8,128)(2,1)} %plane_filter.2), calls=%async_computation.1 | async-start | bytes 4194304 | tf_op jit(solution)/shard_map/all_to_all | solution.py:264
  331.5 1.3 copy-start.1
  332.8 137.1 %all-to-all-start.4 = ((bf16[32,3,24,1024]{3,2,1,0:T(8,128)(2,1)}), bf16[32,3,24,1024]{3,2,1,0:T(8,128)(2,1)}, u32[]{:S(2)}, u32[]{:S(2)}) async-start(bf16[32,3,24,1024]{3,2,1,0:T(8,128)(2,1)} %get-tuple-element.8), calls=%async_computation.4 | async-start | bytes 9437184 | tf_op jit(solution)/shard_map/all_to_all | solution.py:264
  336.9 13.4 %copy-start.6 = (bf16[32,1024]{1,0:T(8,128)(2,1)S(1)}, bf16[32,1024]{1,0:T(8,128)(2,1)}, u32[]{:S(2)}) copy-start(bf16[32,1024]{1,0:T(8,128)(2,1)} %param.17) | copy-start | bytes 196612
  350.4 66.1 %collective-permute-start.7 = (bf16[1,32,1024]{2,1,0:T(8,128)(2,1)S(1)}, bf16[1,32,1024]{2,1,0:T(8,128)(2,1)S(1)}, u32[]{:S(2)}, u32[]{:S(2)}) collective-permute-start(bf16[1,32,1024]{2,1,0:T(8,128)(2,1)S(1)} %get-tuple-element.10), channel_id=1, source_target_pairs={{0,8},{1,9},{2,10},{3,11},{4,12},{5,13},{6,14},{7,15},{8,0},{9,1},... | collective-permute-start | bytes 196616 | tf_op jit(solution)/shard_map/ppermute | solution.py:274
  352.2 94.5 %collective-permute-start.8 = (bf16[1,32,1024]{2,1,0:T(8,128)(2,1)S(1)}, bf16[1,32,1024]{2,1,0:T(8,128)(2,1)S(1)}, u32[]{:S(2)}, u32[]{:S(2)}) collective-permute-start(bf16[1,32,1024]{2,1,0:T(8,128)(2,1)S(1)} %get-tuple-element.10), channel_id=1, source_target_pairs={{0,16},{1,17},{2,18},{3,19},{4,20},{5,21},{6,22},{7,23},{8,24},{9,... | collective-permute-start | bytes 196616 | tf_op jit(solution)/shard_map/ppermute | solution.py:274
  354.6 92.0 %collective-permute-start.9 = (bf16[1,32,1024]{2,1,0:T(8,128)(2,1)S(1)}, bf16[1,32,1024]{2,1,0:T(8,128)(2,1)S(1)}, u32[]{:S(2)}, u32[]{:S(2)}) collective-permute-start(bf16[1,32,1024]{2,1,0:T(8,128)(2,1)S(1)} %get-tuple-element.10), channel_id=1, source_target_pairs={{0,24},{1,25},{2,26},{3,27},{4,28},{5,29},{6,30},{7,31},{8,16},{9,... | collective-permute-start | bytes 196616 | tf_op jit(solution)/shard_map/ppermute | solution.py:274
  446.7 9.2 %collective-permute-start.10 = (bf16[4,32,1024]{2,1,0:T(8,128)(2,1)S(1)}, bf16[4,32,1024]{2,1,0:T(8,128)(2,1)S(1)}, u32[]{:S(2)}, u32[]{:S(2)}) collective-permute-start(bf16[4,32,1024]{2,1,0:T(8,128)(2,1)S(1)} %pad_maximum_fusion.1), channel_id=1, source_target_pairs={{0,2},{1,3},{2,0},{3,1},{4,6},{5,7},{6,4},{7,5},{8,10},{9,11},{10,... | collective-permute-start | bytes 786440 | tf_op jit(solution)/shard_map/ppermute | solution.py:274
  448.0 12.6 %collective-permute-start.11 = (bf16[4,32,1024]{2,1,0:T(8,128)(2,1)S(1)}, bf16[4,32,1024]{2,1,0:T(8,128)(2,1)S(1)}, u32[]{:S(2)}, u32[]{:S(2)}) collective-permute-start(bf16[4,32,1024]{2,1,0:T(8,128)(2,1)S(1)} %pad_maximum_fusion.1), channel_id=1, source_target_pairs={{0,4},{1,5},{2,6},{3,7},{4,0},{5,1},{6,2},{7,3},{8,12},{9,13},{10,... | collective-permute-start | bytes 786440 | tf_op jit(solution)/shard_map/ppermute | solution.py:274
  449.9 11.5 %collective-permute-start.12 = (bf16[4,32,1024]{2,1,0:T(8,128)(2,1)S(1)}, bf16[4,32,1024]{2,1,0:T(8,128)(2,1)S(1)}, u32[]{:S(2)}, u32[]{:S(2)}) collective-permute-start(bf16[4,32,1024]{2,1,0:T(8,128)(2,1)S(1)} %pad_maximum_fusion.1), channel_id=1, source_target_pairs={{0,6},{1,7},{2,4},{3,5},{4,2},{5,3},{6,0},{7,1},{8,14},{9,15},{10,... | collective-permute-start | bytes 786440 | tf_op jit(solution)/shard_map/ppermute | solution.py:274
  462.1 2.7 collective-permute-start.13
  469.9 44.0 %all-to-all-start.3 = ((bf16[32,3,8,1024]{3,2,1,0:T(8,128)(2,1)}), bf16[32,3,8,1024]{3,2,1,0:T(8,128)(2,1)S(1)}, u32[]{:S(2)}, u32[]{:S(2)}) async-start(bf16[32,3,8,1024]{3,2,1,0:T(8,128)(2,1)} %get-tuple-element.7), calls=%async_computation.3 | async-start | bytes 3145728 | tf_op jit(solution)/shard_map/all_to_all | solution.py:264
  513.9 1.2 copy-start.2

commit v3 on v2

--- a/solution.py
+++ b/solution.py
@@ -124,9 +124,9 @@
     out_ref[...] = spec.reshape(out_ref.shape).astype(jnp.bfloat16)
 
 
-def kernel_params(axes):
+def kernel_params(axes, mib=58):
     return pltpu.CompilerParams(
-        dimension_semantics=("arbitrary",) * axes, vmem_limit_bytes=58 * MIB
+        dimension_semantics=("arbitrary",) * axes, vmem_limit_bytes=mib * MIB
     )
 
 
@@ -264,33 +264,36 @@
     return lax.all_to_all(tensor, "sp", split_axis=0, concat_axis=0, tiled=True)
 
 
-def spread(held, bits, devices):
+def combinations(bits):
     deltas = [0]
     for bit in bits:
         deltas = deltas + [delta ^ bit for delta in deltas]
+    return deltas
+
+
+def spread(held, bits, devices):
     blocks = [held]
-    for delta in deltas[1:]:
+    for delta in combinations(bits)[1:]:
         pairs = [(i, i ^ delta) for i in range(devices)]
         blocks.append(lax.ppermute(held, "sp", pairs))
-    return blocks, deltas
-
-
-def gather_blocks(block, stages, devices):
+    return blocks
+
+
+def gather_stages(devices):
+    bits = [1 << at for at in range(devices.bit_length() - 1)]
+    return [bits[3:], bits[1:3], bits[:1]]
+
+
+def in_order(blocks, stages, devices):
     order = [0]
-    held = block[None]
     for bits in stages:
-        blocks, deltas = spread(held, bits, devices)
-        held = jnp.concatenate(blocks, axis=0)
-        order = [slot ^ delta for delta in deltas for slot in order]
+        order = [slot ^ delta for delta in combinations(bits) for slot in order]
     slot_of = jnp.asarray(np.argsort(np.asarray(order)), jnp.int32)
     own = lax.axis_index("sp")
     slots = slot_of[jnp.arange(devices, dtype=jnp.int32) ^ own]
-    return jnp.take(held, slots, axis=0)
-
-
-def gather_stages(devices):
-    bits = [1 << at for at in range(devices.bit_length() - 1)]
-    return [stage for stage in (bits[3:], bits[1:3], bits[:1]) if stage]
+    held = jnp.concatenate(blocks, axis=0)
+    held = held.at[slots].get(mode="promise_in_bounds", wrap_negative_indices=False)
+    return held.reshape(-1, held.shape[-1])
 
 
 def chunks_of(band_count):
@@ -321,16 +324,28 @@
         part = width_forward(table, latents, devices, len(bands))
         pencils.append(exchange(part))
 
-    both = gather_blocks(jnp.concatenate([w_value, w_gate], axis=0), stages, devices)
-    full_value = both[:, :per].reshape(-1, chans)
-    full_gate = both[:, per:].reshape(-1, chans)
+    def joined(blocks, stage):
+        return spread(jnp.concatenate(blocks, axis=0), stages[stage], devices)
+
+    value_blocks = spread(w_value[None], stages[0], devices)
+    for stage in (1, 2):
+        value_blocks = joined(value_blocks, stage)
+    full_value = in_order(value_blocks, stages, devices)
+
+    gate_blocks = spread(w_gate[None], stages[0], devices)
+    gate_blocks = joined(gate_blocks, 1)
 
     taken = jnp.take(embed_table, prompt_ids, axis=1).astype(jnp.float32)
     pooled = jnp.mean(taken, axis=1)
     channel = lax.axis_index("sp") * per + jnp.arange(per, dtype=jnp.int32)
     modulation = 1.0 + pooled + step_embedding(noise_step, channel, chans)
     scaled = (w_out.astype(jnp.float32) * modulation[:, None]).astype(jnp.bfloat16)
-    full_out = gather_blocks(scaled, stages, devices).reshape(-1, chans)
+    out_blocks = spread(scaled[None], stages[0], devices)
+    out_blocks, gate_blocks = lax.optimization_barrier((out_blocks, gate_blocks))
+    full_gate = in_order(joined(gate_blocks, 2), stages, devices)
+    for stage in (1, 2):
+        out_blocks = joined(out_blocks, stage)
+    full_out = in_order(out_blocks, stages, devices)
 
     gain = spectrum.transpose(2, 0, 1, 3).reshape(band_count, TT * HH, chans)
 

time: 526 us -> 519 us (0.987)
    ppermute x14 -> x21, starting transfers between devices: 16 us -> 21.6 us  [spread(): blocks.append(lax.ppermute(held, 'sp', pairs))]
    ppermute x14 -> x21, waiting for transfers between devices: 262 us -> 261 us  [spread(): blocks.append(lax.ppermute(held, 'sp', pairs))]
    unnamed x28 -> x33, local copies, waits for them, and re-layouts: 19.8 us -> 19.7 us
  transfers between devices with their start and end apart: 19 -> 26, of which waited for: 11 -> 13; matrix products, arithmetic and copies ran while one was open for 13% -> 12% of each run, Pallas kernels for 13% -> 13%
where the time goes in v3:
time: 519 us; the launch traced here: 518 us
  waiting for transfers between devices  323 us (62%)
  Pallas kernels  85.7 us (17%)
  local copies, waits for them, and re-layouts  45.6 us (9%)
  starting transfers between devices  45 us (9%)
  matrix products  17.3 us (3%)
    ppermute x21, waiting for transfers between devices, spread(): blocks.append(lax.ppermute(held, 'sp', pairs))  261 us
    all_to_all x5, waiting for transfers between devices, exchange(): return lax.all_to_all(tensor, 'sp', split_axis=0, concat_axis=0, tiled=True)  61.6 us
    pallas_call x2, Pallas kernels, plane_filter(): pl.pallas_call(plane_body, name='plane_filter', grid=(bands,), in_specs=[...  36.5 us
    pallas_call x2, Pallas kernels, finish(): pl.pallas_call(functools.partial(finish_body, len(tables)), name='finish'...  31.7 us
    all_to_all x5, starting transfers between devices, exchange(): return lax.all_to_all(tensor, 'sp', split_axis=0, concat_axis=0, tiled=True)  23.4 us
    ppermute x21, starting transfers between devices, spread(): blocks.append(lax.ppermute(held, 'sp', pairs))  21.6 us
    unnamed x33, local copies, waits for them, and re-layouts  19.7 us
    pallas_call x2, Pallas kernels, width_forward(): pl.pallas_call(forward_body, name='width_forward', grid=(rows // group,),...  17.5 us
  transfers between devices with their start and end apart: 26, of which 13 were waited for; matrix products, arithmetic and copies ran while one was open for 12% of the time, Pallas kernels for 13%

profile of v3, /device:TPU:0, one launch (start us, length us, event | category | flops | bytes accessed | tf_op | source)
XLA Modules:
  0.0 517.7 jit_solution(12290186393320077431)
XLA Ops:
  0.0 6.6 %width_forward.2 = bf16[32,1,32,1024]{3,2,1,0:T(8,128)(2,1)} custom-call(bf16[256,1024]{1,0:T(8,128)(2,1)} %constant.50.clone.table_ref.refs_0_, bf16[4096,1024]{1,0:T(8,128)(2,1)} %refs_5_.3), custom_call_target="tpu_custom_call" | custom-call | flops 2147483648 | bytes 16777216 | tf_op jit(solution)/shard_map/width_forward/pallas_call | solution.py:137
  6.6 7.3 %all-to-all-start = ((bf16[32,1,32,1024]{3,2,1,0:T(8,128)(2,1)}), bf16[32,1,32,1024]{3,2,1,0:T(8,128)(2,1)S(1)}, u32[]{:S(2)}, u32[]{:S(2)}) async-start(bf16[32,1,32,1024]{3,2,1,0:T(8,128)(2,1)} %width_forward.2), calls=%async_computation | async-start | bytes 4194304 | tf_op jit(solution)/shard_map/all_to_all | solution.py:264
  13.9 10.9 %width_forward.3 = bf16[32,3,32,1024]{3,2,1,0:T(8,128)(2,1)} custom-call(bf16[768,1024]{1,0:T(8,128)(2,1)} %constant.51.clone.table_ref.refs_1_, bf16[4096,1024]{1,0:T(8,128)(2,1)} %refs_5_.3), custom_call_target="tpu_custom_call" | custom-call | flops 6442450944 | bytes 16777216 | tf_op jit(solution)/shard_map/width_forward/pallas_call | solution.py:137
  24.8 37.9 %all-to-all-done.pencil_ref = bf16[32,1,32,1024]{3,2,1,0:T(8,128)(2,1)S(1)} async-done(((bf16[32,1,32,1024]{3,2,1,0:T(8,128)(2,1)}), bf16[32,1,32,1024]{3,2,1,0:T(8,128)(2,1)S(1)}, u32[]{:S(2)}, u32[]{:S(2)}) %all-to-all-start) | async-done | bytes 2097184 | tf_op jit(solution)/shard_map/all_to_all | solution.py:264
  62.7 1.3 copy-done.3
  64.0 4.2 all-to-all-start.2
  68.2 3.6 collective-permute-start.2
  71.8 0.8 collective-permute-start
  73.3 103.6 %collective-permute-done.2 = bf16[1,32,1024]{2,1,0:T(8,128)(2,1)S(1)} collective-permute-done((bf16[1,32,1024]{2,1,0:T(8,128)(2,1)S(1)}, bf16[1,32,1024]{2,1,0:T(8,128)(2,1)S(1)}, u32[]{:S(2)}, u32[]{:S(2)}) %collective-permute-start.2) | collective-permute-done | bytes 65568 | tf_op jit(solution)/shard_map/ppermute | solution.py:278
  176.8 36.6 %collective-permute-done.1 = bf16[1,32,1024]{2,1,0:T(8,128)(2,1)S(1)} collective-permute-done((bf16[1,32,1024]{2,1,0:T(8,128)(2,1)S(1)}, bf16[1,32,1024]{2,1,0:T(8,128)(2,1)S(1)}, u32[]{:S(2)}, u32[]{:S(2)}) %collective-permute-start.1) | collective-permute-done | bytes 65568 | tf_op jit(solution)/shard_map/ppermute | solution.py:278
  213.5 1.8 collective-permute-start.5
  215.3 1.7 collective-permute-start.3
  218.9 7.8 %collective-permute-done.3 = bf16[4,32,1024]{2,1,0:T(8,128)(2,1)S(1)} collective-permute-done((bf16[4,32,1024]{2,1,0:T(8,128)(2,1)S(1)}, bf16[4,32,1024]{2,1,0:T(8,128)(2,1)S(1)}, u32[]{:S(2)}, u32[]{:S(2)}) %collective-permute-start.3) | collective-permute-done | bytes 262176 | tf_op jit(solution)/shard_map/ppermute | solution.py:278
  226.7 0.7 constant_dynamic-update-slice_fusion.2
  229.3 9.6 %copy.19 = bf16[4,16,64,1024]{3,2,1,0:T(8,128)(2,1)} copy(bf16[4,16,64,1024]{3,0,2,1:T(4,128)(2,1)} %bitcast.31) | data formatting | bytes 16777216 | tf_op jit(solution)/shard_map/transpose | solution.py:350
  239.8 2.0 gather_fusion.1
  241.8 11.5 %plane_filter.2 = bf16[32,1,32,1024]{3,2,1,0:T(8,128)(2,1)} custom-call(bf16[1024,1024]{1,0:T(8,128)(2,1)} %constant.52.clone.table_ref, bf16[1024,1024]{1,0:T(8,128)(2,1)} %bitcast.34, bf16[4,1024,1024]{2,1,0:T(8,128)(2,1)} %bitcast.32, bf16[32,1,32,1024]{3,2,1,0:T(8,128)(2,1)} %copy-done.3), custom_call_target="tpu_custom_call" | custom-call | flops 6442450944 | bytes 6291456 | tf_op jit(solution)/shard_map/plane_filter/pallas_call | solution.py:185
  253.3 3.7 all-to-all-start.1
  257.0 25.0 %plane_filter.3 = (bf16[32,3,24,1024]{3,2,1,0:T(8,128)(2,1)}, bf16[32,3,8,1024]{3,2,1,0:T(8,128)(2,1)}) custom-call(bf16[1024,1024]{1,0:T(8,128)(2,1)} %constant.52.clone.table_ref, bf16[1024,1024]{1,0:T(8,128)(2,1)} %bitcast.35, bf16[4,1024,1024]{2,1,0:T(8,128)(2,1)} %bitcast.33, bf16[32,3,32,1024]{3,2,1,0:T(8,128)(2,1)} %all-to-all-done.2.pencil_ref), custom_call_target="tpu_custom_call" | custom-call | flops 19327352832 | bytes 18874368 | tf_op jit(solution)/shard_map/plane_filter/pallas_call | solution.py:185
  281.9 23.7 %all-to-all-done.1.refs_2_ = bf16[32,1,32,1024]{3,2,1,0:T(8,128)(2,1)S(1)} async-done(((bf16[32,1,32,1024]{3,2,1,0:T(8,128)(2,1)}), bf16[32,1,32,1024]{3,2,1,0:T(8,128)(2,1)S(1)}, u32[]{:S(2)}, u32[]{:S(2)}) %all-to-all-start.1) | async-done | bytes 2097184 | tf_op jit(solution)/shard_map/all_to_all | solution.py:264
  305.7 1.3 copy-done.1
  307.0 4.1 all-to-all-start.4
  311.1 3.6 collective-permute-start.12
  314.7 0.8 collective-permute-start.10
  316.2 7.4 %copy.20 = bf16[32,32768]{0,1:T(8,128)(2,1)} copy(bf16[32,32768]{1,0:T(8,128)(2,1)} %param.19) | data formatting | bytes 4194304 | tf_op args[5]
  323.6 5.2 %gather_fusion.2 = bf16[256,32]{1,0:T(8,128)(2,1)S(1)} fusion(bf16[32,32768]{0,1:T(8,128)(2,1)} %copy.20, s32[1024]{0:T(1024)S(1)} %pad_clamp_fusion), kind=kCustom, calls=%fused_computation.2 | custom fusion | bytes 33792 | tf_op jit(solution)/shard_map/jit(_take)/gather | solution.py:338
  329.0 65.0 %collective-permute-done.12 = bf16[1,32,1024]{2,1,0:T(8,128)(2,1)S(1)} collective-permute-done((bf16[1,32,1024]{2,1,0:T(8,128)(2,1)S(1)}, bf16[1,32,1024]{2,1,0:T(8,128)(2,1)S(1)}, u32[]{:S(2)}, u32[]{:S(2)}) %collective-permute-start.12) | collective-permute-done | bytes 65568 | tf_op jit(solution)/shard_map/ppermute | solution.py:278
  394.0 27.7 %collective-permute-done.11 = bf16[1,32,1024]{2,1,0:T(8,128)(2,1)S(1)} collective-permute-done((bf16[1,32,1024]{2,1,0:T(8,128)(2,1)S(1)}, bf16[1,32,1024]{2,1,0:T(8,128)(2,1)S(1)}, u32[]{:S(2)}, u32[]{:S(2)}) %collective-permute-start.11) | collective-permute-done | bytes 65568 | tf_op jit(solution)/shard_map/ppermute | solution.py:278
  421.7 2.6 collective-permute-start.15
  424.5 0.7 collective-permute-start.13
  425.3 2.0 collective-permute-start.9
  427.3 4.2 collective-permute-done.9
  431.5 1.6 collective-permute-done.8
  433.1 2.7 collective-permute-done.7
  438.9 2.3 collective-permute-start.19
  441.2 0.8 collective-permute-start.18
  442.5 11.5 %collective-permute-done.17 = bf16[4,32,1024]{2,1,0:T(8,128)(2,1)S(1)} collective-permute-done((bf16[4,32,1024]{2,1,0:T(8,128)(2,1)S(1)}, bf16[4,32,1024]{2,1,0:T(8,128)(2,1)S(1)}, u32[]{:S(2)}, u32[]{:S(2)}) %collective-permute-start.17) | collective-permute-done | bytes 262176 | tf_op jit(solution)/shard_map/ppermute | solution.py:278
  454.0 0.9 constant_dynamic-update-slice_fusion.26
  454.9 0.9 constant_dynamic-update-slice_fusion.25
  455.8 0.9 constant_dynamic-update-slice_fusion.24
  456.7 2.0 gather_fusion.3
  458.7 4.1 all-to-all-start.3
  462.9 17.3 %fusion.3.refs_4_ = bf16[4096,1024]{1,0:T(8,128)(2,1)} fusion(bf16[4096,1024]{1,0:T(8,128)(2,1)} %refs_5_.3, bf16[1024,1024]{1,0:T(8,128)(2,1)} %bitcast.36), kind=kOutput, calls=%fused_computation.10 | convolution fusion | flops 8610906112 | bytes 18874368 | tf_op jit(solution)/shard_map/dot_general | solution.py:358
  480.2 1.1 constant_dynamic-update-slice_fusion.31
  481.3 3.6 gather_fusion.4
  484.9 22.3 %finish.2.refs_7_ = bf16[4096,1024]{1,0:T(8,128)(2,1)} custom-call(bf16[256,1024]{1,0:T(8,128)(2,1)} %constant.50.clone.table_ref.refs_0_, bf16[768,1024]{1,0:T(8,128)(2,1)} %constant.51.clone.table_ref.refs_1_, bf16[32,1,32,1024]{3,2,1,0:T(8,128)(2,1)} %copy-done.1, bf16[32,3,24,1024]{3,2,1,0:T(8,128)(2,1)} %all-to-all-done.4.refs_3_, ...), custom_call_target="tpu_custom_call" | custom-call | flops 12884901888 | bytes 25165824 | tf_op jit(solution)/shard_map/finish/pallas_call | solution.py:240
  507.2 1.1 copy-done.2
  508.3 9.4 %finish.3 = bf16[4096,1024]{1,0:T(8,128)(2,1)} custom-call(bf16[256,1024]{1,0:T(8,128)(2,1)} %constant.50.clone.table_ref.refs_0_, bf16[768,1024]{1,0:T(8,128)(2,1)} %constant.51.clone.table_ref.refs_1_, bf16[32,1,32,1024]{3,2,1,0:T(8,128)(2,1)} %copy-done.1, bf16[32,3,8,1024]{3,2,1,0:T(8,128)(2,1)} %copy-done.2, ...), custom_call_target="tpu_custom_call", output_to_operand_aliasing={{}: (7, {})} | custom-call | flops 4294967296 | bytes 8388608 | tf_op jit(solution)/shard_map/finish/pallas_call | solution.py:240
  (67 shorter events, 9.5 us)
Async XLA Ops:
  6.6 56.1 %all-to-all-start = ((bf16[32,1,32,1024]{3,2,1,0:T(8,128)(2,1)}), bf16[32,1,32,1024]{3,2,1,0:T(8,128)(2,1)S(1)}, u32[]{:S(2)}, u32[]{:S(2)}) async-start(bf16[32,1,32,1024]{3,2,1,0:T(8,128)(2,1)} %width_forward.2), calls=%async_computation | async-start | bytes 4194304 | tf_op jit(solution)/shard_map/all_to_all | solution.py:264
  24.8 43.4 %copy-start.4 = (bf16[32,1024]{1,0:T(8,128)(2,1)S(1)}, bf16[32,1024]{1,0:T(8,128)(2,1)}, u32[]{:S(2)}) copy-start(bf16[32,1024]{1,0:T(8,128)(2,1)} %param.16) | copy-start | bytes 196612
  62.7 1.3 copy-start.3
  64.0 189.3 %all-to-all-start.2 = ((bf16[32,3,32,1024]{3,2,1,0:T(8,128)(2,1)}), bf16[32,3,32,1024]{3,2,1,0:T(8,128)(2,1)}, u32[]{:S(2)}, u32[]{:S(2)}) async-start(bf16[32,3,32,1024]{3,2,1,0:T(8,128)(2,1)} %width_forward.3), calls=%async_computation.2 | async-start | bytes 12582912 | tf_op jit(solution)/shard_map/all_to_all | solution.py:264
  68.2 108.6 %collective-permute-start.2 = (bf16[1,32,1024]{2,1,0:T(8,128)(2,1)S(1)}, bf16[1,32,1024]{2,1,0:T(8,128)(2,1)S(1)}, u32[]{:S(2)}, u32[]{:S(2)}) collective-permute-start(bf16[1,32,1024]{2,1,0:T(8,128)(2,1)S(1)} %bitcast.37), channel_id=1, source_target_pairs={{0,24},{1,25},{2,26},{3,27},{4,28},{5,29},{6,30},{7,31},{8,16},{9,... | collective-permute-start | bytes 196616 | tf_op jit(solution)/shard_map/ppermute | solution.py:278
  71.8 141.6 %collective-permute-start.1 = (bf16[1,32,1024]{2,1,0:T(8,128)(2,1)S(1)}, bf16[1,32,1024]{2,1,0:T(8,128)(2,1)S(1)}, u32[]{:S(2)}, u32[]{:S(2)}) collective-permute-start(bf16[1,32,1024]{2,1,0:T(8,128)(2,1)S(1)} %bitcast.38), channel_id=1, source_target_pairs={{0,16},{1,17},{2,18},{3,19},{4,20},{5,21},{6,22},{7,23},{8,24},{9,... | collective-permute-start | bytes 196616 | tf_op jit(solution)/shard_map/ppermute | solution.py:278
  71.8 141.6 %collective-permute-start = (bf16[1,32,1024]{2,1,0:T(8,128)(2,1)S(1)}, bf16[1,32,1024]{2,1,0:T(8,128)(2,1)S(1)}, u32[]{:S(2)}, u32[]{:S(2)}) collective-permute-start(bf16[1,32,1024]{2,1,0:T(8,128)(2,1)S(1)} %bitcast.39), channel_id=1, source_target_pairs={{0,8},{1,9},{2,10},{3,11},{4,12},{5,13},{6,14},{7,15},{8,0},{9,1},... | collective-permute-start | bytes 196616 | tf_op jit(solution)/shard_map/ppermute | solution.py:278
  213.5 15.1 %collective-permute-start.5 = (bf16[4,32,1024]{2,1,0:T(8,128)(2,1)S(1)}, bf16[4,32,1024]{2,1,0:T(8,128)(2,1)S(1)}, u32[]{:S(2)}, u32[]{:S(2)}) collective-permute-start(bf16[4,32,1024]{2,1,0:T(8,128)(2,1)S(1)} %pad_maximum_fusion.1), channel_id=1, source_target_pairs={{0,6},{1,7},{2,4},{3,5},{4,2},{5,3},{6,0},{7,1},{8,14},{9,15},{10,... | collective-permute-start | bytes 786440 | tf_op jit(solution)/shard_map/ppermute | solution.py:278
  215.3 12.6 %collective-permute-start.4 = (bf16[4,32,1024]{2,1,0:T(8,128)(2,1)S(1)}, bf16[4,32,1024]{2,1,0:T(8,128)(2,1)S(1)}, u32[]{:S(2)}, u32[]{:S(2)}) collective-permute-start(bf16[4,32,1024]{2,1,0:T(8,128)(2,1)S(1)} %pad_maximum_fusion.1), channel_id=1, source_target_pairs={{0,4},{1,5},{2,6},{3,7},{4,0},{5,1},{6,2},{7,3},{8,12},{9,13},{10,... | collective-permute-start | bytes 786440 | tf_op jit(solution)/shard_map/ppermute | solution.py:278
  215.3 11.4 %collective-permute-start.3 = (bf16[4,32,1024]{2,1,0:T(8,128)(2,1)S(1)}, bf16[4,32,1024]{2,1,0:T(8,128)(2,1)S(1)}, u32[]{:S(2)}, u32[]{:S(2)}) collective-permute-start(bf16[4,32,1024]{2,1,0:T(8,128)(2,1)S(1)} %pad_maximum_fusion.1), channel_id=1, source_target_pairs={{0,2},{1,3},{2,0},{3,1},{4,6},{5,7},{6,4},{7,5},{8,10},{9,11},{10,... | collective-permute-start | bytes 786440 | tf_op jit(solution)/shard_map/ppermute | solution.py:278
  229.3 10.4 %collective-permute-start.6 = (bf16[16,32,1024]{2,1,0:T(8,128)(2,1)}, bf16[16,32,1024]{2,1,0:T(8,128)(2,1)S(1)}, u32[]{:S(2)}, u32[]{:S(2)}) collective-permute-start(bf16[16,32,1024]{2,1,0:T(8,128)(2,1)} %get-tuple-element.31), channel_id=1, source_target_pairs={{0,1},{1,0},{2,3},{3,2},{4,5},{5,4},{6,7},{7,6},{8,9},{9,8},{10,11... | collective-permute-start | bytes 3145736 | tf_op jit(solution)/shard_map/ppermute | solution.py:278
  229.3 9.7 %copy-start = (s32[32]{0:T(128)S(1)}, s32[32]{0:T(128)}, u32[]{:S(2)}) copy-start(s32[32]{0:T(128)} %constant.53.clone) | copy-start | bytes 388
  253.3 52.3 %all-to-all-start.1 = ((bf16[32,1,32,1024]{3,2,1,0:T(8,128)(2,1)}), bf16[32,1,32,1024]{3,2,1,0:T(8,128)(2,1)S(1)}, u32[]{:S(2)}, u32[]{:S(2)}) async-start(bf16[32,1,32,1024]{3,2,1,0:T(8,128)(2,1)} %plane_filter.2), calls=%async_computation.1 | async-start | bytes 4194304 | tf_op jit(solution)/shard_map/all_to_all | solution.py:264
  305.7 1.3 copy-start.1
  305.7 5.4 %copy-start.6 = (bf16[32,1024]{1,0:T(8,128)(2,1)S(1)}, bf16[32,1024]{1,0:T(8,128)(2,1)}, u32[]{:S(2)}) copy-start(bf16[32,1024]{1,0:T(8,128)(2,1)} %param.17) | copy-start | bytes 196612
  307.0 151.8 %all-to-all-start.4 = ((bf16[32,3,24,1024]{3,2,1,0:T(8,128)(2,1)}), bf16[32,3,24,1024]{3,2,1,0:T(8,128)(2,1)}, u32[]{:S(2)}, u32[]{:S(2)}) async-start(bf16[32,3,24,1024]{3,2,1,0:T(8,128)(2,1)} %get-tuple-element.24), calls=%async_computation.4 | async-start | bytes 9437184 | tf_op jit(solution)/shard_map/all_to_all | solution.py:264
  311.1 82.9 %collective-permute-start.12 = (bf16[1,32,1024]{2,1,0:T(8,128)(2,1)S(1)}, bf16[1,32,1024]{2,1,0:T(8,128)(2,1)S(1)}, u32[]{:S(2)}, u32[]{:S(2)}) collective-permute-start(bf16[1,32,1024]{2,1,0:T(8,128)(2,1)S(1)} %bitcast.41), channel_id=1, source_target_pairs={{0,24},{1,25},{2,26},{3,27},{4,28},{5,29},{6,30},{7,31},{8,16},{9,... | collective-permute-start | bytes 196616 | tf_op jit(solution)/shard_map/ppermute | solution.py:278
  314.7 107.0 %collective-permute-start.11 = (bf16[1,32,1024]{2,1,0:T(8,128)(2,1)S(1)}, bf16[1,32,1024]{2,1,0:T(8,128)(2,1)S(1)}, u32[]{:S(2)}, u32[]{:S(2)}) collective-permute-start(bf16[1,32,1024]{2,1,0:T(8,128)(2,1)S(1)} %bitcast.42), channel_id=1, source_target_pairs={{0,16},{1,17},{2,18},{3,19},{4,20},{5,21},{6,22},{7,23},{8,24},{9,... | collective-permute-start | bytes 196616 | tf_op jit(solution)/shard_map/ppermute | solution.py:278
  314.7 107.0 %collective-permute-start.10 = (bf16[1,32,1024]{2,1,0:T(8,128)(2,1)S(1)}, bf16[1,32,1024]{2,1,0:T(8,128)(2,1)S(1)}, u32[]{:S(2)}, u32[]{:S(2)}) collective-permute-start(bf16[1,32,1024]{2,1,0:T(8,128)(2,1)S(1)} %bitcast.43), channel_id=1, source_target_pairs={{0,8},{1,9},{2,10},{3,11},{4,12},{5,13},{6,14},{7,15},{8,0},{9,1},... | collective-permute-start | bytes 196616 | tf_op jit(solution)/shard_map/ppermute | solution.py:278
  316.2 7.4 %copy-start.7 = (s32[256]{0:T(256)S(1)}, s32[256]{0:T(256)}, u32[]{:S(2)}) copy-start(s32[256]{0:T(256)} %param.20) | copy-start | bytes 3076
  316.2 109.1 %copy-start.5 = (bf16[32,1024]{1,0:T(8,128)(2,1)S(1)}, bf16[32,1024]{1,0:T(8,128)(2,1)}, u32[]{:S(2)}) copy-start(bf16[32,1024]{1,0:T(8,128)(2,1)} %param.18) | copy-start | bytes 196612
  421.7 14.1 %collective-permute-start.15 = (bf16[4,32,1024]{2,1,0:T(8,128)(2,1)S(1)}, bf16[4,32,1024]{2,1,0:T(8,128)(2,1)S(1)}, u32[]{:S(2)}, u32[]{:S(2)}) collective-permute-start(bf16[4,32,1024]{2,1,0:T(8,128)(2,1)S(1)} %pad_maximum_fusion.2), channel_id=1, source_target_pairs={{0,6},{1,7},{2,4},{3,5},{4,2},{5,3},{6,0},{7,1},{8,14},{9,15},{10,... | collective-permute-start | bytes 786440 | tf_op jit(solution)/shard_map/ppermute | solution.py:278
  424.3 11.7 %collective-permute-start.14 = (bf16[4,32,1024]{2,1,0:T(8,128)(2,1)S(1)}, bf16[4,32,1024]{2,1,0:T(8,128)(2,1)S(1)}, u32[]{:S(2)}, u32[]{:S(2)}) collective-permute-start(bf16[4,32,1024]{2,1,0:T(8,128)(2,1)S(1)} %pad_maximum_fusion.2), channel_id=1, source_target_pairs={{0,4},{1,5},{2,6},{3,7},{4,0},{5,1},{6,2},{7,3},{8,12},{9,13},{10,... | collective-permute-start | bytes 786440 | tf_op jit(solution)/shard_map/ppermute | solution.py:278
  424.5 11.5 %collective-permute-start.13 = (bf16[4,32,1024]{2,1,0:T(8,128)(2,1)S(1)}, bf16[4,32,1024]{2,1,0:T(8,128)(2,1)S(1)}, u32[]{:S(2)}, u32[]{:S(2)}) collective-permute-start(bf16[4,32,1024]{2,1,0:T(8,128)(2,1)S(1)} %pad_maximum_fusion.2), channel_id=1, source_target_pairs={{0,2},{1,3},{2,0},{3,1},{4,6},{5,7},{6,4},{7,5},{8,10},{9,11},{10,... | collective-permute-start | bytes 786440 | tf_op jit(solution)/shard_map/ppermute | solution.py:278
  425.3 6.2 %collective-permute-start.9 = (bf16[1,32,1024]{2,1,0:T(8,128)(2,1)S(1)}, bf16[1,32,1024]{2,1,0:T(8,128)(2,1)S(1)}, u32[]{:S(2)}, u32[]{:S(2)}) collective-permute-start(bf16[1,32,1024]{2,1,0:T(8,128)(2,1)S(1)} %fusion.4), channel_id=1, source_target_pairs={{0,24},{1,25},{2,26},{3,27},{4,28},{5,29},{6,30},{7,31},{8,16},{9,... | collective-permute-start | bytes 196616 | tf_op jit(solution)/shard_map/ppermute | solution.py:278
  427.3 5.8 %collective-permute-start.8 = (bf16[1,32,1024]{2,1,0:T(8,128)(2,1)S(1)}, bf16[1,32,1024]{2,1,0:T(8,128)(2,1)S(1)}, u32[]{:S(2)}, u32[]{:S(2)}) collective-permute-start(bf16[1,32,1024]{2,1,0:T(8,128)(2,1)S(1)} %fusion.4), channel_id=1, source_target_pairs={{0,16},{1,17},{2,18},{3,19},{4,20},{5,21},{6,22},{7,23},{8,24},{9,... | collective-permute-start | bytes 196616 | tf_op jit(solution)/shard_map/ppermute | solution.py:278
  431.5 4.3 collective-permute-start.7
  436.2 20.5 %collective-permute-start.16 = (bf16[16,32,1024]{2,1,0:T(8,128)(2,1)S(1)}, bf16[16,32,1024]{2,1,0:T(8,128)(2,1)S(1)}, u32[]{:S(2)}, u32[]{:S(2)}) collective-permute-start(bf16[16,32,1024]{2,1,0:T(8,128)(2,1)S(1)} %pad_maximum_fusion), channel_id=1, source_target_pairs={{0,1},{1,0},{2,3},{3,2},{4,5},{5,4},{6,7},{7,6},{8,9},{9,8},{10,11... | collective-permute-start | bytes 3145736 | tf_op jit(solution)/shard_map/ppermute | solution.py:278
  438.9 16.9 %collective-permute-start.19 = (bf16[4,32,1024]{2,1,0:T(8,128)(2,1)S(1)}, bf16[4,32,1024]{2,1,0:T(8,128)(2,1)S(1)}, u32[]{:S(2)}, u32[]{:S(2)}) collective-permute-start(bf16[4,32,1024]{2,1,0:T(8,128)(2,1)S(1)} %get-tuple-element.39), channel_id=1, source_target_pairs={{0,6},{1,7},{2,4},{3,5},{4,2},{5,3},{6,0},{7,1},{8,14},{9,15},{10,... | collective-permute-start | bytes 786440 | tf_op jit(solution)/shard_map/ppermute | solution.py:278
  441.2 13.7 %collective-permute-start.18 = (bf16[4,32,1024]{2,1,0:T(8,128)(2,1)S(1)}, bf16[4,32,1024]{2,1,0:T(8,128)(2,1)S(1)}, u32[]{:S(2)}, u32[]{:S(2)}) collective-permute-start(bf16[4,32,1024]{2,1,0:T(8,128)(2,1)S(1)} %get-tuple-element.39), channel_id=1, source_target_pairs={{0,4},{1,5},{2,6},{3,7},{4,0},{5,1},{6,2},{7,3},{8,12},{9,13},{10,... | collective-permute-start | bytes 786440 | tf_op jit(solution)/shard_map/ppermute | solution.py:278
  442.1 11.9 %collective-permute-start.17 = (bf16[4,32,1024]{2,1,0:T(8,128)(2,1)S(1)}, bf16[4,32,1024]{2,1,0:T(8,128)(2,1)S(1)}, u32[]{:S(2)}, u32[]{:S(2)}) collective-permute-start(bf16[4,32,1024]{2,1,0:T(8,128)(2,1)S(1)} %get-tuple-element.39), channel_id=1, source_target_pairs={{0,2},{1,3},{2,0},{3,1},{4,6},{5,7},{6,4},{7,5},{8,10},{9,11},{10,... | collective-permute-start | bytes 786440 | tf_op jit(solution)/shard_map/ppermute | solution.py:278
  456.6 23.5 %collective-permute-start.20 = (bf16[16,32,1024]{2,1,0:T(8,128)(2,1)}, bf16[16,32,1024]{2,1,0:T(8,128)(2,1)S(1)}, u32[]{:S(2)}, u32[]{:S(2)}) collective-permute-start(bf16[16,32,1024]{2,1,0:T(8,128)(2,1)} %get-tuple-element.25), channel_id=1, source_target_pairs={{0,1},{1,0},{2,3},{3,2},{4,5},{5,4},{6,7},{7,6},{8,9},{9,8},{10,11... | collective-permute-start | bytes 3145736 | tf_op jit(solution)/shard_map/ppermute | solution.py:278
  458.7 48.4 %all-to-all-start.3 = ((bf16[32,3,8,1024]{3,2,1,0:T(8,128)(2,1)}), bf16[32,3,8,1024]{3,2,1,0:T(8,128)(2,1)S(1)}, u32[]{:S(2)}, u32[]{:S(2)}) async-start(bf16[32,3,8,1024]{3,2,1,0:T(8,128)(2,1)} %get-tuple-element.15), calls=%async_computation.3 | async-start | bytes 3145728 | tf_op jit(solution)/shard_map/all_to_all | solution.py:264
  507.2 1.1 copy-start.2

commit v4 on v2

--- a/solution.py
+++ b/solution.py
@@ -89,6 +89,7 @@
 
 
 SUB = 8
+NEAR = 8
 MIB = 1 << 20
 
 
@@ -153,11 +154,11 @@
     )(table, latents)
 
 
-def plane_body(table_ref, value_ref, spectrum_ref, pencil_ref, *rest):
+def plane_body(own_ref, table_ref, value_ref, spectrum_ref, pencil_ref, *rest):
     out_refs, (first_ref, second_ref) = rest[:-2], rest[-2:]
     cells, chans = first_ref.shape
-    step = min(cells, 256)
     lines = pencil_ref.shape[2]
+    step = NEAR * lines
     pencil = pencil_ref[...].reshape(cells, chans)
     for at in range(0, cells, step):
         part = pl.ds(at, step)
@@ -167,43 +168,51 @@
         full = dot32(first_ref[part, :], value_ref[...])
         gain = spectrum_ref[0, part, :].astype(jnp.float32)
         second_ref[part, :] = (full * gain).astype(jnp.bfloat16)
-    per = step // lines
-    for at in range(0, cells, step):
-        back = dot32(table_ref[pl.ds(at, step), :], second_ref[...])
-        back = back.reshape(per, lines, chans).astype(jnp.bfloat16)
-        line = 0
-        for out_ref in out_refs:
-            count = out_ref.shape[2]
-            out_ref[pl.ds(at // lines, per), 0] = back[:, line : line + count]
-            line += count
-
-
-def plane_filter(table, w_value, spectrum, pencil, first_band, splits):
+    keep = out_refs[0].shape[2]
+    for plane in range(cells // step):
+        back = dot32(table_ref[pl.ds(plane * step, step), :], second_ref[...])
+        back = back.reshape(NEAR, lines, chans).astype(jnp.bfloat16)
+        out_refs[0][pl.ds(plane * NEAR, NEAR), 0] = back[:, :keep]
+        if len(out_refs) == 2:
+            for near in range(NEAR):
+                out_refs[1][near ^ (own_ref[0] % NEAR), plane ^ (own_ref[0] // NEAR), 0] = back[
+                    near, keep:
+                ]
+
+
+def plane_filter(own, table, w_value, spectrum, pencil, first_band, keep):
     devices, bands, lines, chans = pencil.shape
     cells = devices * lines
-    block = lambda count: pl.BlockSpec((devices, 1, count, chans), lambda j: (0, j, 0, 0))
+    block = lambda count: pl.BlockSpec((devices, 1, count, chans), lambda j, own: (0, j, 0, 0))
+    out_specs = [block(keep)]
+    out_shape = [jax.ShapeDtypeStruct((devices, bands, keep, chans), jnp.bfloat16)]
+    if keep < lines:
+        lead, tail = (NEAR, devices // NEAR), (lines - keep, chans)
+        out_specs.append(pl.BlockSpec(lead + (1,) + tail, lambda j, own: (0, 0, j, 0, 0)))
+        out_shape.append(jax.ShapeDtypeStruct(lead + (bands,) + tail, jnp.bfloat16))
     return pl.pallas_call(
         plane_body,
         name="plane_filter",
-        grid=(bands,),
-        in_specs=[
-            pl.BlockSpec(table.shape, lambda j: (0, 0)),
-            pl.BlockSpec(w_value.shape, lambda j: (0, 0)),
-            pl.BlockSpec((1, cells, chans), lambda j: (first_band + j, 0, 0)),
-            block(lines),
-        ],
-        out_specs=[block(count) for count in splits],
-        out_shape=[
-            jax.ShapeDtypeStruct((devices, bands, count, chans), jnp.bfloat16) for count in splits
-        ],
-        scratch_shapes=[pltpu.VMEM((cells, chans), jnp.bfloat16)] * 2,
+        grid_spec=pltpu.PrefetchScalarGridSpec(
+            num_scalar_prefetch=1,
+            grid=(bands,),
+            in_specs=[
+                pl.BlockSpec(table.shape, lambda j, own: (0, 0)),
+                pl.BlockSpec(w_value.shape, lambda j, own: (0, 0)),
+                pl.BlockSpec((1, cells, chans), lambda j, own: (first_band + j, 0, 0)),
+                block(lines),
+            ],
+            out_specs=out_specs,
+            scratch_shapes=[pltpu.VMEM((cells, chans), jnp.bfloat16)] * 2,
+        ),
+        out_shape=out_shape,
         compiler_params=kernel_params(1),
         cost_estimate=pl.CostEstimate(
             flops=2 * bands * cells * chans * (2 * cells + chans),
             bytes_accessed=6 * bands * cells * chans,
             transcendentals=0,
         ),
-    )(table, w_value, spectrum, pencil)
+    )(own, table, w_value, spectrum, pencil)
 
 
 def finish_body(parts, *refs):
@@ -260,8 +269,84 @@
     )(*inputs)
 
 
+def tail_body(own_ref, *refs):
+    first_table, rest_table, first_ref = refs[:3]
+    far = len(refs) - 11
+    parts = refs[3 : 3 + far]
+    gate_ref, latents_ref, w_out_ref, _, out_ref, first_held, rest_wide, rest_held = refs[3 + far :]
+
+    @pl.when(pl.program_id(0) == 0)
+    def _():
+        wide = first_ref[...].astype(jnp.float32).reshape(first_held.shape)
+        first_held[...] = wide.astype(jnp.bfloat16)
+        for offset, part in enumerate(parts):
+            plane = offset ^ (own_ref[0] // NEAR)
+            for near in range(NEAR):
+                source = plane * NEAR + (near ^ (own_ref[0] % NEAR))
+                block = part[near].astype(jnp.float32)
+                rest_wide[source] = block.reshape(rest_wide.shape[1:])
+        rest_held[...] = rest_wide[...].reshape(rest_held.shape).astype(jnp.bfloat16)
+
+    mix = dot32(first_table[...], first_held[...], (0, 0))
+    mix = mix + dot32(rest_table[...], rest_held[...], (0, 0))
+    mixed = (mix * gate_ref[...].astype(jnp.float32)).astype(jnp.bfloat16)
+    out = latents_ref[...].astype(jnp.float32) + dot32(mixed, w_out_ref[...])
+    out_ref[...] = out.astype(jnp.bfloat16)
+
+
+def finish_tail(own, tables, first, parts, gate, latents, w_out, group_at, done):
+    rows, chans = latents.shape
+    devices = first.shape[0]
+    bands = parts[0].shape[1]
+    group = SUB * WW
+    pieces = 4
+    piece = group // pieces
+    by_piece = pl.BlockSpec((piece, chans), lambda s, own: (group_at * pieces + s, 0))
+    inputs = [own, *tables, first, *parts, gate, latents, w_out, done]
+    return pl.pallas_call(
+        tail_body,
+        name="finish_tail",
+        grid_spec=pltpu.PrefetchScalarGridSpec(
+            num_scalar_prefetch=1,
+            grid=(pieces,),
+            in_specs=[
+                pl.BlockSpec((table.shape[0], piece), lambda s, own: (0, s)) for table in tables
+            ]
+            + [pl.BlockSpec(first.shape[:2] + (SUB, chans), lambda s, own: (0, 0, group_at, 0))]
+            + [pl.BlockSpec(part.shape, lambda s, own: (0, 0, 0, 0)) for part in parts]
+            + [by_piece, by_piece, pl.BlockSpec(w_out.shape, lambda s, own: (0, 0))]
+            + [pl.BlockSpec(memory_space=pl.ANY)],
+            out_specs=by_piece,
+            scratch_shapes=[
+                pltpu.VMEM((tables[0].shape[0], chans), jnp.bfloat16),
+                pltpu.VMEM((devices, bands * SUB, chans), jnp.float32),
+                pltpu.VMEM((tables[1].shape[0], chans), jnp.bfloat16),
+            ],
+        ),
+        out_shape=jax.ShapeDtypeStruct((rows, chans), jnp.bfloat16),
+        input_output_aliases={len(inputs) - 1: 0},
+        compiler_params=kernel_params(1),
+        cost_estimate=pl.CostEstimate(
+            flops=2 * group * chans * (group + chans),
+            bytes_accessed=8 * group * chans,
+            transcendentals=0,
+        ),
+    )(*inputs)
+
+
+def relay(tail, devices):
+    shift = lambda part, delta: spread_one(part, delta, devices)
+    came = [tail[0]] + [shift(tail[near], near) for near in range(1, NEAR)]
+    together = [jnp.stack([part[far] for part in came]) for far in range(devices // NEAR)]
+    return together[:1] + [shift(part, far * NEAR) for far, part in enumerate(together) if far]
+
+
 def exchange(tensor):
     return lax.all_to_all(tensor, "sp", split_axis=0, concat_axis=0, tiled=True)
+
+
+def spread_one(held, delta, devices):
+    return lax.ppermute(held, "sp", [(i, i ^ delta) for i in range(devices)])
 
 
 def spread(held, bits, devices):
@@ -270,8 +355,7 @@
         deltas = deltas + [delta ^ bit for delta in deltas]
     blocks = [held]
     for delta in deltas[1:]:
-        pairs = [(i, i ^ delta) for i in range(devices)]
-        blocks.append(lax.ppermute(held, "sp", pairs))
+        blocks.append(spread_one(held, delta, devices))
     return blocks, deltas
 
 
@@ -290,15 +374,11 @@
 
 def gather_stages(devices):
     bits = [1 << at for at in range(devices.bit_length() - 1)]
-    return [stage for stage in (bits[3:], bits[1:3], bits[:1]) if stage]
+    return [bits[3:], bits[1:3], bits[:1]]
 
 
 def chunks_of(band_count):
     return [(0,)] + ([tuple(range(1, band_count))] if band_count > 1 else [])
-
-
-def splits_of(lines):
-    return [lines - SUB, SUB] if lines > SUB else [lines]
 
 
 def local_planes(devices, *args):
@@ -310,8 +390,10 @@
     band_count = spectrum.shape[2]
     lines = row_count // WW
     chunks = chunks_of(band_count)
-    splits = splits_of(lines)
+    keep = lines - SUB
     stages = gather_stages(devices)
+    each_far = [[bit] for bit in reversed(stages[0])] + stages[1:]
+    own = lax.axis_index("sp").astype(jnp.int32)
     tables = [jnp.asarray(width_table(devices, band_count, bands)) for bands in chunks]
     plane = jnp.asarray(plane_table())
     per = w_value.shape[0]
@@ -327,32 +409,24 @@
 
     taken = jnp.take(embed_table, prompt_ids, axis=1).astype(jnp.float32)
     pooled = jnp.mean(taken, axis=1)
-    channel = lax.axis_index("sp") * per + jnp.arange(per, dtype=jnp.int32)
+    channel = own * per + jnp.arange(per, dtype=jnp.int32)
     modulation = 1.0 + pooled + step_embedding(noise_step, channel, chans)
     scaled = (w_out.astype(jnp.float32) * modulation[:, None]).astype(jnp.bfloat16)
-    full_out = gather_blocks(scaled, stages, devices).reshape(-1, chans)
+    full_out = gather_blocks(scaled, each_far, devices).reshape(-1, chans)
 
     gain = spectrum.transpose(2, 0, 1, 3).reshape(band_count, TT * HH, chans)
 
-    returned = []
-    for at, (pencil, bands) in enumerate(zip(pencils, chunks)):
-        last = at == len(chunks) - 1
-        parts = plane_filter(plane, full_value, gain, pencil, bands[0], splits if last else [lines])
-        returned.append([exchange(part) for part in parts])
+    (first,) = plane_filter(own[None], plane, full_value, gain, pencils[0], 0, lines)
+    first = exchange(first)
+    rest, tail = plane_filter(own[None], plane, full_value, gain, pencils[1], 1, keep)
+    rest = exchange(rest)
+    tail = relay(tail, devices)
 
     gate_rows = jnp.dot(latents, full_gate, preferred_element_type=jnp.float32)
     gate = jax.nn.silu(gate_rows).astype(jnp.bfloat16)
 
-    done, line = None, 0
-    for piece, count in enumerate(splits):
-        spectra = [back[min(piece, len(back) - 1)] for back in returned]
-        starts = [0 if len(back) == 1 else line // SUB for back in returned]
-        done = finish(
-            tables, spectra, starts, gate, latents, full_out,
-            (line // SUB, count // SUB), done,
-        )
-        line += count
-    return done
+    done = finish(tables, [first, rest], [0, 0], gate, latents, full_out, (0, keep // SUB))
+    return finish_tail(own[None], tables, first, tail, gate, latents, full_out, keep // SUB, done)
 
 
 def solution(mesh):
@@ -368,8 +442,14 @@
     )
     devices = mesh.shape["sp"]
     lines = TT * HH // devices
-    whole_channels = mesh.shape["ch"] == 1 and devices & (devices - 1) == 0 and lines % SUB == 0
-    local = functools.partial(local_planes, devices) if whole_channels else local_split_channels
+    in_planes = (
+        mesh.shape["ch"] == 1
+        and devices >= 2 * NEAR
+        and devices & (devices - 1) == 0
+        and WW >= 2 * devices
+        and lines >= 2 * SUB
+    )
+    local = functools.partial(local_planes, devices) if in_planes else local_split_channels
     return jax.shard_map(
         local, mesh=mesh, in_specs=placed, out_specs=P(("grp", "sp", "ch"), None), check_vma=False
     )

time: 526 us -> 560 us (1.065)
  waiting for transfers between devices: 324 us -> 348 us
    ppermute x14 -> x23, waiting for transfers between devices: 262 us -> 287 us  [spread_one(): return lax.ppermute(held, 'sp', [(i, i ^ delta) for i in range(devices)])]
    pallas_call x2 -> x3, Pallas kernels: 36.5 us -> 46.1 us  [the longest x2 36.5 us: plane_filter(): pl.pallas_call(plane_body, name='plane_filter', grid_spec=pltpu.PrefetchS...]
    pallas_call x2 -> x1, Pallas kernels: 31.7 us -> 22.3 us  [finish(): pl.pallas_call(functools.partial(finish_body, len(tables)), name='finish'...]
    ppermute x14 -> x23, starting transfers between devices: 16 us -> 24 us  [spread_one(): return lax.ppermute(held, 'sp', [(i, i ^ delta) for i in range(devices)])]
    all_to_all x5 -> x4, starting transfers between devices: 25.7 us -> 21.3 us  [exchange(): return lax.all_to_all(tensor, 'sp', split_axis=0, concat_axis=0, tiled=True)]
    unnamed x28 -> x46, local copies, waits for them, and re-layouts: 19.8 us -> 19.4 us
    all_to_all x5 -> x4, waiting for transfers between devices: 61.5 us -> 61.5 us  [exchange(): return lax.all_to_all(tensor, 'sp', split_axis=0, concat_axis=0, tiled=True)]
  transfers between devices with their start and end apart: 19 -> 27, of which waited for: 11 -> 15; matrix products, arithmetic and copies ran while one was open for 13% -> 12% of each run, Pallas kernels for 13% -> 13%
where the time goes in v4:
time: 560 us; the launch traced here: 553 us
  waiting for transfers between devices  348 us (62%)
  Pallas kernels  85.9 us (15%)
  local copies, waits for them, and re-layouts  50.2 us (9%)
  starting transfers between devices  45.3 us (8%)
  matrix products  17.1 us (3%)
    ppermute x23, waiting for transfers between devices, spread_one(): return lax.ppermute(held, 'sp', [(i, i ^ delta) for i in range(devices)])  287 us
    all_to_all x4, waiting for transfers between devices, exchange(): return lax.all_to_all(tensor, 'sp', split_axis=0, concat_axis=0, tiled=True)  61.5 us
    pallas_call x2, Pallas kernels, plane_filter(): pl.pallas_call(plane_body, name='plane_filter', grid_spec=pltpu.PrefetchS...  36.5 us
    ppermute x23, starting transfers between devices, spread_one(): return lax.ppermute(held, 'sp', [(i, i ^ delta) for i in range(devices)])  24 us
    pallas_call x1, Pallas kernels, finish(): pl.pallas_call(functools.partial(finish_body, len(tables)), name='finish'...  22.3 us
    all_to_all x4, starting transfers between devices, exchange(): return lax.all_to_all(tensor, 'sp', split_axis=0, concat_axis=0, tiled=True)  21.3 us
    unnamed x46, local copies, waits for them, and re-layouts  19.4 us
    pallas_call x2, Pallas kernels, width_forward(): pl.pallas_call(forward_body, name='width_forward', grid=(rows // group,),...  17.5 us
  transfers between devices with their start and end apart: 27, of which 15 were waited for; matrix products, arithmetic and copies ran while one was open for 12% of the time, Pallas kernels for 13%

profile of v4, /device:TPU:0, one launch (start us, length us, event | category | flops | bytes accessed | tf_op | source)
XLA Modules:
  0.0 553.1 jit_solution(14120199440308609031)
XLA Ops:
  0.0 6.6 %width_forward.2 = bf16[32,1,32,1024]{3,2,1,0:T(8,128)(2,1)} custom-call(bf16[256,1024]{1,0:T(8,128)(2,1)} %constant.77.clone.table_ref.refs_0_, bf16[4096,1024]{1,0:T(8,128)(2,1)} %refs_8_.1), custom_call_target="tpu_custom_call" | custom-call | flops 2147483648 | bytes 16777216 | tf_op jit(solution)/shard_map/width_forward/pallas_call | solution.py:138
  6.6 7.3 %all-to-all-start = ((bf16[32,1,32,1024]{3,2,1,0:T(8,128)(2,1)}), bf16[32,1,32,1024]{3,2,1,0:T(8,128)(2,1)S(1)}, u32[]{:S(2)}, u32[]{:S(2)}) async-start(bf16[32,1,32,1024]{3,2,1,0:T(8,128)(2,1)} %width_forward.2), calls=%async_computation | async-start | bytes 4194304 | tf_op jit(solution)/shard_map/all_to_all | solution.py:345
  13.9 10.9 %width_forward.3 = bf16[32,3,32,1024]{3,2,1,0:T(8,128)(2,1)} custom-call(bf16[768,1024]{1,0:T(8,128)(2,1)} %constant.78.clone.table_ref.refs_1_, bf16[4096,1024]{1,0:T(8,128)(2,1)} %refs_8_.1), custom_call_target="tpu_custom_call" | custom-call | flops 6442450944 | bytes 16777216 | tf_op jit(solution)/shard_map/width_forward/pallas_call | solution.py:138
  24.8 37.9 %all-to-all-done.pencil_ref = bf16[32,1,32,1024]{3,2,1,0:T(8,128)(2,1)S(1)} async-done(((bf16[32,1,32,1024]{3,2,1,0:T(8,128)(2,1)}), bf16[32,1,32,1024]{3,2,1,0:T(8,128)(2,1)S(1)}, u32[]{:S(2)}, u32[]{:S(2)}) %all-to-all-start) | async-done | bytes 2097184 | tf_op jit(solution)/shard_map/all_to_all | solution.py:345
  62.7 1.4 copy-done.3
  64.0 4.2 all-to-all-start.2
  68.3 1.8 collective-permute-start
  70.0 2.4 collective-permute-start.1
  72.7 102.0 %collective-permute-done = bf16[1,64,1024]{2,1,0:T(8,128)(2,1)S(1)} collective-permute-done((bf16[1,64,1024]{2,1,0:T(8,128)(2,1)S(1)}, bf16[1,64,1024]{2,1,0:T(8,128)(2,1)S(1)}, u32[]{:S(2)}, u32[]{:S(2)}) %collective-permute-start) | collective-permute-done | bytes 131104 | tf_op jit(solution)/shard_map/ppermute | solution.py:349
  174.7 42.2 %collective-permute-done.1 = bf16[1,64,1024]{2,1,0:T(8,128)(2,1)S(1)} collective-permute-done((bf16[1,64,1024]{2,1,0:T(8,128)(2,1)S(1)}, bf16[1,64,1024]{2,1,0:T(8,128)(2,1)S(1)}, u32[]{:S(2)}, u32[]{:S(2)}) %collective-permute-start.1) | collective-permute-done | bytes 131104 | tf_op jit(solution)/shard_map/ppermute | solution.py:349
  217.3 2.0 collective-permute-start.4
  220.0 1.2 collective-permute-start.5
  223.5 8.4 %collective-permute-done.3 = bf16[4,64,1024]{2,1,0:T(8,128)(2,1)S(1)} collective-permute-done((bf16[4,64,1024]{2,1,0:T(8,128)(2,1)S(1)}, bf16[4,64,1024]{2,1,0:T(8,128)(2,1)S(1)}, u32[]{:S(2)}, u32[]{:S(2)}) %collective-permute-start.3) | collective-permute-done | bytes 524320 | tf_op jit(solution)/shard_map/ppermute | solution.py:349
  232.9 8.4 %collective-permute-done.4 = bf16[4,64,1024]{2,1,0:T(8,128)(2,1)S(1)} collective-permute-done((bf16[4,64,1024]{2,1,0:T(8,128)(2,1)S(1)}, bf16[4,64,1024]{2,1,0:T(8,128)(2,1)S(1)}, u32[]{:S(2)}, u32[]{:S(2)}) %collective-permute-start.4) | collective-permute-done | bytes 524320 | tf_op jit(solution)/shard_map/ppermute | solution.py:349
  243.7 9.7 %copy.18 = bf16[4,16,64,1024]{3,2,1,0:T(8,128)(2,1)} copy(bf16[4,16,64,1024]{3,0,2,1:T(4,128)(2,1)} %bitcast.64) | data formatting | bytes 16777216 | tf_op jit(solution)/shard_map/transpose | solution.py:417
  254.1 1.5 constant_dynamic-update-slice_fusion.7
  255.6 5.0 gather_fusion.1
  260.6 2.6 broadcast_select_fusion
  263.3 2.5 fusion.14
  265.8 11.5 %plane_filter.2 = bf16[32,1,32,1024]{3,2,1,0:T(8,128)(2,1)} custom-call(s32[1]{0:T(128)} %bitcast.own_ref, bf16[1024,1024]{1,0:T(8,128)(2,1)} %constant.79.clone.table_ref, bf16[1024,1024]{1,0:T(8,128)(2,1)} %bitcast.68, bf16[4,1024,1024]{2,1,0:T(8,128)(2,1)} %bitcast.65, bf16[32,1,32,1024]{3,2,1,0:T(8,128)(2,1)} %copy-done.3), custom_call_target="tpu_custom_call" | custom-call | flops 6442450944 | bytes 6291456 | tf_op jit(solution)/shard_map/plane_filter/pallas_call | solution.py:193
  277.2 5.7 %all-to-all-start.1 = ((bf16[32,1,32,1024]{3,2,1,0:T(8,128)(2,1)}), bf16[32,1,32,1024]{3,2,1,0:T(8,128)(2,1)S(1)}, u32[]{:S(2)}, u32[]{:S(2)}) async-start(bf16[32,1,32,1024]{3,2,1,0:T(8,128)(2,1)} %plane_filter.2), calls=%async_computation.1 | async-start | bytes 4194304 | tf_op jit(solution)/shard_map/all_to_all | solution.py:345
  283.0 25.0 %plane_filter.3 = (bf16[32,3,24,1024]{3,2,1,0:T(8,128)(2,1)}, bf16[8,4,3,8,1024]{4,3,2,1,0:T(8,128)(2,1)}) custom-call(s32[1]{0:T(128)} %bitcast.own_ref, bf16[1024,1024]{1,0:T(8,128)(2,1)} %constant.79.clone.table_ref, bf16[1024,1024]{1,0:T(8,128)(2,1)} %bitcast.69, bf16[4,1024,1024]{2,1,0:T(8,128)(2,1)} %bitcast.66, ...), custom_call_target="tpu_custom_call" | custom-call | flops 19327352832 | bytes 18874368 | tf_op jit(solution)/shard_map/plane_filter/pallas_call | solution.py:193
  308.0 23.7 %all-to-all-done.1.refs_2_ = bf16[32,1,32,1024]{3,2,1,0:T(8,128)(2,1)S(1)} async-done(((bf16[32,1,32,1024]{3,2,1,0:T(8,128)(2,1)}), bf16[32,1,32,1024]{3,2,1,0:T(8,128)(2,1)S(1)}, u32[]{:S(2)}, u32[]{:S(2)}) %all-to-all-start.1) | async-done | bytes 2097184 | tf_op jit(solution)/shard_map/all_to_all | solution.py:345
  331.6 1.3 copy-done.2
  332.9 4.1 all-to-all-start.3
  337.1 7.4 %copy.20 = bf16[32,32768]{0,1:T(8,128)(2,1)} copy(bf16[32,32768]{1,0:T(8,128)(2,1)} %param.18) | data formatting | bytes 4194304 | tf_op args[5]
  345.1 5.2 gather_fusion.3
  350.6 2.7 collective-permute-start.17
  353.2 91.6 %collective-permute-done.17 = bf16[1,32,1024]{2,1,0:T(8,128)(2,1)S(1)} collective-permute-done((bf16[1,32,1024]{2,1,0:T(8,128)(2,1)S(1)}, bf16[1,32,1024]{2,1,0:T(8,128)(2,1)S(1)}, u32[]{:S(2)}, u32[]{:S(2)}) %collective-permute-start.17) | collective-permute-done | bytes 65568 | tf_op jit(solution)/shard_map/ppermute | solution.py:349
  444.9 5.0 collective-permute-done.18
  449.9 1.3 collective-permute-start.19
  451.9 1.8 collective-permute-start.20
  455.4 3.2 collective-permute-done.19
  459.4 4.5 collective-permute-done.20
  466.3 1.8 collective-permute-done.22
  469.1 2.3 gather_fusion.4
  471.4 1.7 bitcast_select_fusion.refs_6_.refs_9_
  473.5 17.1 %fusion.3.refs_4_.refs_7_ = bf16[4096,1024]{1,0:T(8,128)(2,1)} fusion(bf16[4096,1024]{1,0:T(8,128)(2,1)} %refs_8_.1, bf16[1024,1024]{1,0:T(8,128)(2,1)S(1)} %bitcast.67), kind=kOutput, calls=%fused_computation.10 | convolution fusion | flops 8610906112 | bytes 18874368 | tf_op jit(solution)/shard_map/dot_general | solution.py:425
  491.0 1.6 collective-permute-start.9
  492.7 1.7 collective-permute-start.10
  494.5 1.5 collective-permute-start.12
  496.0 2.7 collective-permute-done.8
  498.8 3.0 collective-permute-done.9
  501.8 10.0 %collective-permute-done.11 = bf16[4,3,8,1024]{3,2,1,0:T(8,128)(2,1)S(1)} collective-permute-done((bf16[4,3,8,1024]{3,2,1,0:T(8,128)(2,1)S(1)}, bf16[4,3,8,1024]{3,2,1,0:T(8,128)(2,1)S(1)}, u32[]{:S(2)}, u32[]{:S(2)}) %collective-permute-start.11) | collective-permute-done | bytes 196640 | tf_op jit(solution)/shard_map/ppermute | solution.py:349
  512.8 2.7 collective-permute-start.15
  516.4 22.3 %finish.1.refs_10_ = bf16[4096,1024]{1,0:T(8,128)(2,1)} custom-call(bf16[256,1024]{1,0:T(8,128)(2,1)} %constant.77.clone.table_ref.refs_0_, bf16[768,1024]{1,0:T(8,128)(2,1)} %constant.78.clone.table_ref.refs_1_, bf16[32,1,32,1024]{3,2,1,0:T(8,128)(2,1)} %copy-done.2, bf16[32,3,24,1024]{3,2,1,0:T(8,128)(2,1)} %all-to-all-done.3.refs_3_, ...), custom_call_target="tpu_custom_call" | custom-call | flops 12884901888 | bytes 25165824 | tf_op jit(solution)/shard_map/finish/pallas_call | solution.py:249
  538.7 3.9 collective-permute-done.15.refs_5_
  543.5 9.6 %finish_tail.1 = bf16[4096,1024]{1,0:T(8,128)(2,1)} custom-call(s32[1]{0:T(128)} %bitcast.own_ref, bf16[256,1024]{1,0:T(8,128)(2,1)} %constant.77.clone.table_ref.refs_0_, bf16[768,1024]{1,0:T(8,128)(2,1)} %constant.78.clone.table_ref.refs_1_, bf16[32,1,32,1024]{3,2,1,0:T(8,128)(2,1)} %copy-done.2, ...), custom_call_target="tpu_custom_call", output_to_operand_aliasing={{}: (11, {})} | custom-call | flops 4294967296 | bytes 8388608 | tf_op jit(solution)/shard_map/finish_tail/pallas_call | solution.py:306
  (94 shorter events, 18.5 us)
Async XLA Ops:
  6.6 56.1 %all-to-all-start = ((bf16[32,1,32,1024]{3,2,1,0:T(8,128)(2,1)}), bf16[32,1,32,1024]{3,2,1,0:T(8,128)(2,1)S(1)}, u32[]{:S(2)}, u32[]{:S(2)}) async-start(bf16[32,1,32,1024]{3,2,1,0:T(8,128)(2,1)} %width_forward.2), calls=%async_computation | async-start | bytes 4194304 | tf_op jit(solution)/shard_map/all_to_all | solution.py:345
  24.8 43.4 %copy-start.10 = (bf16[32,1024]{1,0:T(8,128)(2,1)S(1)}, bf16[32,1024]{1,0:T(8,128)(2,1)}, u32[]{:S(2)}) copy-start(bf16[32,1024]{1,0:T(8,128)(2,1)} %param.16) | copy-start | bytes 196612
  24.8 43.4 %copy-start.11 = (bf16[32,1024]{1,0:T(8,128)(2,1)S(1)}, bf16[32,1024]{1,0:T(8,128)(2,1)}, u32[]{:S(2)}) copy-start(bf16[32,1024]{1,0:T(8,128)(2,1)} %param.15) | copy-start | bytes 196612
  62.7 1.4 copy-start.3
  64.0 213.2 %all-to-all-start.2 = ((bf16[32,3,32,1024]{3,2,1,0:T(8,128)(2,1)}), bf16[32,3,32,1024]{3,2,1,0:T(8,128)(2,1)}, u32[]{:S(2)}, u32[]{:S(2)}) async-start(bf16[32,3,32,1024]{3,2,1,0:T(8,128)(2,1)} %width_forward.3), calls=%async_computation.2 | async-start | bytes 12582912 | tf_op jit(solution)/shard_map/all_to_all | solution.py:345
  68.3 106.4 %collective-permute-start = (bf16[1,64,1024]{2,1,0:T(8,128)(2,1)S(1)}, bf16[1,64,1024]{2,1,0:T(8,128)(2,1)S(1)}, u32[]{:S(2)}, u32[]{:S(2)}) collective-permute-start(bf16[1,64,1024]{2,1,0:T(8,128)(2,1)S(1)} %maximum_bitcast_fusion), channel_id=1, source_target_pairs={{0,8},{1,9},{2,10},{3,11},{4,12},{5,13},{6,14},{7,15},{8,0},{9,1},... | collective-permute-start | bytes 393224 | tf_op jit(solution)/shard_map/ppermute | solution.py:349
  70.0 146.8 %collective-permute-start.1 = (bf16[1,64,1024]{2,1,0:T(8,128)(2,1)S(1)}, bf16[1,64,1024]{2,1,0:T(8,128)(2,1)S(1)}, u32[]{:S(2)}, u32[]{:S(2)}) collective-permute-start(bf16[1,64,1024]{2,1,0:T(8,128)(2,1)S(1)} %maximum_bitcast_fusion), channel_id=1, source_target_pairs={{0,16},{1,17},{2,18},{3,19},{4,20},{5,21},{6,22},{7,23},{8,24},{9,... | collective-permute-start | bytes 393224 | tf_op jit(solution)/shard_map/ppermute | solution.py:349
  72.5 144.4 %collective-permute-start.2 = (bf16[1,64,1024]{2,1,0:T(8,128)(2,1)S(1)}, bf16[1,64,1024]{2,1,0:T(8,128)(2,1)S(1)}, u32[]{:S(2)}, u32[]{:S(2)}) collective-permute-start(bf16[1,64,1024]{2,1,0:T(8,128)(2,1)S(1)} %maximum_bitcast_fusion), channel_id=1, source_target_pairs={{0,24},{1,25},{2,26},{3,27},{4,28},{5,29},{6,30},{7,31},{8,16},{9,... | collective-permute-start | bytes 393224 | tf_op jit(solution)/shard_map/ppermute | solution.py:349
  217.0 14.9 %collective-permute-start.3 = (bf16[4,64,1024]{2,1,0:T(8,128)(2,1)S(1)}, bf16[4,64,1024]{2,1,0:T(8,128)(2,1)S(1)}, u32[]{:S(2)}, u32[]{:S(2)}) collective-permute-start(bf16[4,64,1024]{2,1,0:T(8,128)(2,1)S(1)} %pad_maximum_fusion), channel_id=1, source_target_pairs={{0,2},{1,3},{2,0},{3,1},{4,6},{5,7},{6,4},{7,5},{8,10},{9,11},{10,... | collective-permute-start | bytes 1572872 | tf_op jit(solution)/shard_map/ppermute | solution.py:349
  217.3 24.0 %collective-permute-start.4 = (bf16[4,64,1024]{2,1,0:T(8,128)(2,1)S(1)}, bf16[4,64,1024]{2,1,0:T(8,128)(2,1)S(1)}, u32[]{:S(2)}, u32[]{:S(2)}) collective-permute-start(bf16[4,64,1024]{2,1,0:T(8,128)(2,1)S(1)} %pad_maximum_fusion), channel_id=1, source_target_pairs={{0,4},{1,5},{2,6},{3,7},{4,0},{5,1},{6,2},{7,3},{8,12},{9,13},{10,... | collective-permute-start | bytes 1572872 | tf_op jit(solution)/shard_map/ppermute | solution.py:349
  220.0 22.5 %collective-permute-start.5 = (bf16[4,64,1024]{2,1,0:T(8,128)(2,1)S(1)}, bf16[4,64,1024]{2,1,0:T(8,128)(2,1)S(1)}, u32[]{:S(2)}, u32[]{:S(2)}) collective-permute-start(bf16[4,64,1024]{2,1,0:T(8,128)(2,1)S(1)} %pad_maximum_fusion), channel_id=1, source_target_pairs={{0,6},{1,7},{2,4},{3,5},{4,2},{5,3},{6,0},{7,1},{8,14},{9,15},{10,... | collective-permute-start | bytes 1572872 | tf_op jit(solution)/shard_map/ppermute | solution.py:349
  243.7 10.4 %collective-permute-start.6 = (bf16[16,64,1024]{2,1,0:T(8,128)(2,1)}, bf16[16,64,1024]{2,1,0:T(8,128)(2,1)S(1)}, u32[]{:S(2)}, u32[]{:S(2)}) collective-permute-start(bf16[16,64,1024]{2,1,0:T(8,128)(2,1)} %get-tuple-element.24), channel_id=1, source_target_pairs={{0,1},{1,0},{2,3},{3,2},{4,5},{5,4},{6,7},{7,6},{8,9},{9,8},{10,11... | collective-permute-start | bytes 6291464 | tf_op jit(solution)/shard_map/ppermute | solution.py:349
  243.7 9.7 %copy-start.13 = (s32[256]{0:T(256)S(1)}, s32[256]{0:T(256)}, u32[]{:S(2)}) copy-start(s32[256]{0:T(256)} %param.19) | copy-start | bytes 3076
  243.7 9.7 %copy-start.1 = (s32[32]{0:T(128)S(1)}, s32[32]{0:T(128)}, u32[]{:S(2)}) copy-start(s32[32]{0:T(128)} %constant.80.clone) | copy-start | bytes 388
  277.2 54.4 %all-to-all-start.1 = ((bf16[32,1,32,1024]{3,2,1,0:T(8,128)(2,1)}), bf16[32,1,32,1024]{3,2,1,0:T(8,128)(2,1)S(1)}, u32[]{:S(2)}, u32[]{:S(2)}) async-start(bf16[32,1,32,1024]{3,2,1,0:T(8,128)(2,1)} %plane_filter.2), calls=%async_computation.1 | async-start | bytes 4194304 | tf_op jit(solution)/shard_map/all_to_all | solution.py:345
  331.6 1.3 copy-start.2
  332.9 183.4 %all-to-all-start.3 = ((bf16[32,3,24,1024]{3,2,1,0:T(8,128)(2,1)}), bf16[32,3,24,1024]{3,2,1,0:T(8,128)(2,1)}, u32[]{:S(2)}, u32[]{:S(2)}) async-start(bf16[32,3,24,1024]{3,2,1,0:T(8,128)(2,1)} %get-tuple-element.8), calls=%async_computation.3 | async-start | bytes 9437184 | tf_op jit(solution)/shard_map/all_to_all | solution.py:345
  337.0 13.4 %copy-start.12 = (bf16[32,1024]{1,0:T(8,128)(2,1)S(1)}, bf16[32,1024]{1,0:T(8,128)(2,1)}, u32[]{:S(2)}) copy-start(bf16[32,1024]{1,0:T(8,128)(2,1)} %param.17) | copy-start | bytes 196612
  350.3 115.1 %copy-start = (s32[32]{0:T(128)S(1)}, s32[32]{0:T(128)}, u32[]{:S(2)}) copy-start(s32[32]{0:T(128)} %constant.81.clone) | copy-start | bytes 388
  350.6 94.2 %collective-permute-start.17 = (bf16[1,32,1024]{2,1,0:T(8,128)(2,1)S(1)}, bf16[1,32,1024]{2,1,0:T(8,128)(2,1)S(1)}, u32[]{:S(2)}, u32[]{:S(2)}) collective-permute-start(bf16[1,32,1024]{2,1,0:T(8,128)(2,1)S(1)} %get-tuple-element.10), channel_id=1, source_target_pairs={{0,16},{1,17},{2,18},{3,19},{4,20},{5,21},{6,22},{7,23},{8,24},{9,... | collective-permute-start | bytes 196616 | tf_op jit(solution)/shard_map/ppermute | solution.py:349
  444.8 5.0 collective-permute-start.18
  449.9 8.7 %collective-permute-start.19 = (bf16[4,32,1024]{2,1,0:T(8,128)(2,1)S(1)}, bf16[4,32,1024]{2,1,0:T(8,128)(2,1)S(1)}, u32[]{:S(2)}, u32[]{:S(2)}) collective-permute-start(bf16[4,32,1024]{2,1,0:T(8,128)(2,1)S(1)} %pad_maximum_fusion.1), channel_id=1, source_target_pairs={{0,2},{1,3},{2,0},{3,1},{4,6},{5,7},{6,4},{7,5},{8,10},{9,11},{10,... | collective-permute-start | bytes 786440 | tf_op jit(solution)/shard_map/ppermute | solution.py:349
  451.9 12.0 %collective-permute-start.20 = (bf16[4,32,1024]{2,1,0:T(8,128)(2,1)S(1)}, bf16[4,32,1024]{2,1,0:T(8,128)(2,1)S(1)}, u32[]{:S(2)}, u32[]{:S(2)}) collective-permute-start(bf16[4,32,1024]{2,1,0:T(8,128)(2,1)S(1)} %pad_maximum_fusion.1), channel_id=1, source_target_pairs={{0,4},{1,5},{2,6},{3,7},{4,0},{5,1},{6,2},{7,3},{8,12},{9,13},{10,... | collective-permute-start | bytes 786440 | tf_op jit(solution)/shard_map/ppermute | solution.py:349
  454.3 10.3 %collective-permute-start.21 = (bf16[4,32,1024]{2,1,0:T(8,128)(2,1)S(1)}, bf16[4,32,1024]{2,1,0:T(8,128)(2,1)S(1)}, u32[]{:S(2)}, u32[]{:S(2)}) collective-permute-start(bf16[4,32,1024]{2,1,0:T(8,128)(2,1)S(1)} %pad_maximum_fusion.1), channel_id=1, source_target_pairs={{0,6},{1,7},{2,4},{3,5},{4,2},{5,3},{6,0},{7,1},{8,14},{9,15},{10,... | collective-permute-start | bytes 786440 | tf_op jit(solution)/shard_map/ppermute | solution.py:349
  465.4 2.7 collective-permute-start.22
  471.4 2.1 copy-start.4
  473.5 17.1 %copy-start.5 = (bf16[8,4,3,8,1024]{4,3,2,1,0:T(8,128)(2,1)S(1)}, bf16[8,4,3,8,1024]{4,3,2,1,0:T(8,128)(2,1)}, u32[]{:S(2)}) copy-start(bf16[8,4,3,8,1024]{4,3,2,1,0:T(8,128)(2,1)} %get-tuple-element.7) | copy-start | bytes 4718596
  490.7 3.7 collective-permute-start.7
  491.0 7.8 %collective-permute-start.8 = (bf16[4,3,8,1024]{3,2,1,0:T(8,128)(2,1)S(1)}, bf16[4,3,8,1024]{3,2,1,0:T(8,128)(2,1)S(1)}, u32[]{:S(2)}, u32[]{:S(2)}) collective-permute-start(bf16[4,3,8,1024]{3,2,1,0:T(8,128)(2,1)S(1)} %get-tuple-element.22), channel_id=1, source_target_pairs={{0,2},{1,3},{2,0},{3,1},{4,6},{5,7},{6,4},{7,5},{8,10},{9,11},{10,... | collective-permute-start | bytes 589832 | tf_op jit(solution)/shard_map/ppermute | solution.py:349
  491.0 10.7 %collective-permute-start.9 = (bf16[4,3,8,1024]{3,2,1,0:T(8,128)(2,1)S(1)}, bf16[4,3,8,1024]{3,2,1,0:T(8,128)(2,1)S(1)}, u32[]{:S(2)}, u32[]{:S(2)}) collective-permute-start(bf16[4,3,8,1024]{3,2,1,0:T(8,128)(2,1)S(1)} %get-tuple-element.21), channel_id=1, source_target_pairs={{0,3},{1,2},{2,1},{3,0},{4,7},{5,6},{6,5},{7,4},{8,11},{9,10},{10,... | collective-permute-start | bytes 589832 | tf_op jit(solution)/shard_map/ppermute | solution.py:349
  492.7 9.1 %collective-permute-start.10 = (bf16[4,3,8,1024]{3,2,1,0:T(8,128)(2,1)S(1)}, bf16[4,3,8,1024]{3,2,1,0:T(8,128)(2,1)S(1)}, u32[]{:S(2)}, u32[]{:S(2)}) collective-permute-start(bf16[4,3,8,1024]{3,2,1,0:T(8,128)(2,1)S(1)} %get-tuple-element.20), channel_id=1, source_target_pairs={{0,4},{1,5},{2,6},{3,7},{4,0},{5,1},{6,2},{7,3},{8,12},{9,13},{10,... | collective-permute-start | bytes 589832 | tf_op jit(solution)/shard_map/ppermute | solution.py:349
  494.4 17.4 %collective-permute-start.11 = (bf16[4,3,8,1024]{3,2,1,0:T(8,128)(2,1)S(1)}, bf16[4,3,8,1024]{3,2,1,0:T(8,128)(2,1)S(1)}, u32[]{:S(2)}, u32[]{:S(2)}) collective-permute-start(bf16[4,3,8,1024]{3,2,1,0:T(8,128)(2,1)S(1)} %get-tuple-element.19), channel_id=1, source_target_pairs={{0,5},{1,4},{2,7},{3,6},{4,1},{5,0},{6,3},{7,2},{8,13},{9,12},{10,... | collective-permute-start | bytes 589832 | tf_op jit(solution)/shard_map/ppermute | solution.py:349
  494.5 17.3 %collective-permute-start.12 = (bf16[4,3,8,1024]{3,2,1,0:T(8,128)(2,1)S(1)}, bf16[4,3,8,1024]{3,2,1,0:T(8,128)(2,1)S(1)}, u32[]{:S(2)}, u32[]{:S(2)}) collective-permute-start(bf16[4,3,8,1024]{3,2,1,0:T(8,128)(2,1)S(1)} %get-tuple-element.18), channel_id=1, source_target_pairs={{0,6},{1,7},{2,4},{3,5},{4,2},{5,3},{6,0},{7,1},{8,14},{9,15},{10,... | collective-permute-start | bytes 589832 | tf_op jit(solution)/shard_map/ppermute | solution.py:349
  498.7 13.1 %collective-permute-start.13 = (bf16[4,3,8,1024]{3,2,1,0:T(8,128)(2,1)S(1)}, bf16[4,3,8,1024]{3,2,1,0:T(8,128)(2,1)S(1)}, u32[]{:S(2)}, u32[]{:S(2)}) collective-permute-start(bf16[4,3,8,1024]{3,2,1,0:T(8,128)(2,1)S(1)} %get-tuple-element.17), channel_id=1, source_target_pairs={{0,7},{1,6},{2,5},{3,4},{4,3},{5,2},{6,1},{7,0},{8,15},{9,14},{10,... | collective-permute-start | bytes 589832 | tf_op jit(solution)/shard_map/ppermute | solution.py:349
  511.9 26.8 %copy-start.6 = (bf16[8,3,8,1024]{3,2,1,0:T(8,128)(2,1)}, bf16[8,3,8,1024]{3,2,1,0:T(8,128)(2,1)S(1)}, u32[]{:S(2)}) copy-start(bf16[8,3,8,1024]{3,2,1,0:T(8,128)(2,1)S(1)} %get-tuple-element.39.refs_3_) | copy-start | bytes 1179652
  511.9 26.8 %collective-permute-start.14 = (bf16[8,3,8,1024]{3,2,1,0:T(8,128)(2,1)S(1)}, bf16[8,3,8,1024]{3,2,1,0:T(8,128)(2,1)S(1)}, u32[]{:S(2)}, u32[]{:S(2)}) collective-permute-start(bf16[8,3,8,1024]{3,2,1,0:T(8,128)(2,1)S(1)} %get-tuple-element.38), channel_id=1, source_target_pairs={{0,8},{1,9},{2,10},{3,11},{4,12},{5,13},{6,14},{7,15},{8,0},{9,1},... | collective-permute-start | bytes 1179656 | tf_op jit(solution)/shard_map/ppermute | solution.py:349
  512.8 29.8 %collective-permute-start.15 = (bf16[8,3,8,1024]{3,2,1,0:T(8,128)(2,1)S(1)}, bf16[8,3,8,1024]{3,2,1,0:T(8,128)(2,1)S(1)}, u32[]{:S(2)}, u32[]{:S(2)}) collective-permute-start(bf16[8,3,8,1024]{3,2,1,0:T(8,128)(2,1)S(1)} %get-tuple-element.37), channel_id=1, source_target_pairs={{0,16},{1,17},{2,18},{3,19},{4,20},{5,21},{6,22},{7,23},{8,24},{9,... | collective-permute-start | bytes 1179656 | tf_op jit(solution)/shard_map/ppermute | solution.py:349
  515.5 27.1 %collective-permute-start.16 = (bf16[8,3,8,1024]{3,2,1,0:T(8,128)(2,1)S(1)}, bf16[8,3,8,1024]{3,2,1,0:T(8,128)(2,1)S(1)}, u32[]{:S(2)}, u32[]{:S(2)}) collective-permute-start(bf16[8,3,8,1024]{3,2,1,0:T(8,128)(2,1)S(1)} %get-tuple-element.36), channel_id=1, source_target_pairs={{0,24},{1,25},{2,26},{3,27},{4,28},{5,29},{6,30},{7,31},{8,16},{9,... | collective-permute-start | bytes 1179656 | tf_op jit(solution)/shard_map/ppermute | solution.py:349
  538.7 3.9 copy-start.7
  542.6 0.8 copy-start.8
  542.6 0.9 copy-start.9
